TPU v7x, 32 devices: a whole 2x2x4 slice. The times are simulated.
32 devices in a mesh: seq: 8 (over z, y), mp: 4 (over x, core).
Axes of the slice: x: 2, y: 2, z: 4, core: 2. Of those that a mesh axis runs over, the one named last changes fastest.
Arguments:
- resid: bfloat16 [2048, 5120], P('seq', 'mp'), may hold values from -15 to 15
- queries: bfloat16 [2048, 5120], P('seq', 'mp'), may hold values from -28 to 28
- keys: bfloat16 [2048, 5120], P('seq', 'mp'), may hold values from -12.25 to 12.25
- values: bfloat16 [2048, 5120], P('seq', 'mp'), may hold values from -6 to 6
- doc_ids: int32 [2048], P('seq'), may hold values from 0 to 3, as said below
- out_proj: bfloat16 [5120, 5120], P('mp'), may hold values from -0.5 to 0.5
- ffn_gain: bfloat16 [5120], P('mp'), may hold values from 0.25 to 1.75
- w_in: bfloat16 [5120, 13824], P('mp', 'seq'), may hold values from -0.078125 to 0.078125
- w_out: bfloat16 [13824, 5120], P('seq', 'mp'), may hold values from -0.109375 to 0.109375
- hot_index: int32 [8, 384], P('seq'), may hold values from 0 to 1727, as said below
- hot_blocks: int32 [8], P('seq'), may hold values from 1 to 3, as said below
Outputs:
- layer_out: bfloat16 [2048, 5120], P('seq', 'mp')
- hot_mean: float32 [8, 384], P('seq')
Inputs may be any that keep to these rules, and one draw needn't show every extreme that they name: `doc_ids`: document numbers never fall along the tokens; every number from 0 to 3 occurs; some document has 1024 tokens. `hot_index`: row g holds 384 distinct neuron numbers of group g; only its first 128 * hot_blocks[g] entries are live, the others are ignored. `hot_blocks`: some group has exactly 3 live blocks.
All inputs are finite; a program needn't handle non-finite values.
Results may differ from a plain program's by a relative error of at most 0.014.
Values may be sent and summed in bfloat16 or wider, within the bound.
A program may use at most 192 MiB of HBM per device.

v0:
```python
import functools

import jax
import jax.numpy as jnp
from jax import lax
from jax.experimental import pallas as pl
from jax.experimental.pallas import tpu as pltpu
from jax.sharding import PartitionSpec as P

HEAD_DIM = 128
BLOCK = 128
MESH = pl.DeviceIdType.MESH
VMEM = pltpu.VMEM

epsilon = 1e-05
masked_score = -1e30


def row_length(mesh):
    seq = mesh.shape["seq"]
    try:
        first = [mesh.devices[i, 0].coords for i in range(seq)]
        size = len({c[1] for c in first})
        if seq % size == 0:
            return size
    except (AttributeError, IndexError, TypeError):
        pass
    return 2


def gather_kernel(nz, ny, up, down, window, chunks, count, *refs):
    ins = refs[:count]
    outs = refs[count : 2 * count]
    sems = refs[2 * count :]
    own_sem, zs_sem, zr_sem, ys_sem, yr_sem = sems
    me = lax.axis_index("seq")
    mp = lax.axis_index("mp")
    z = me // ny
    y = me % ny

    def dev(zz, yy):
        return (zz * ny + yy, mp)

    barrier = pltpu.get_barrier_semaphore()
    for step in (-1, 1):
        ok = (z + step >= 0) & (z + step < nz)

        @pl.when(ok)
        def _(step=step):
            pl.semaphore_signal(barrier, inc=1, device_id=dev(z + step, y), device_id_type=MESH)

    for dy in range(1, ny):
        pl.semaphore_signal(
            barrier, inc=1, device_id=dev(z, (y + dy) % ny), device_id_type=MESH
        )
    below = jnp.where(z > 0, 1, 0)
    above = jnp.where(z < nz - 1, 1, 0)
    pl.semaphore_wait(barrier, below + above + ny - 1)

    def piece(ref, a, c):
        rows = ins[a].shape[0]
        if chunks[a] == 1:
            return ref
        size = rows // chunks[a]
        return ref.at[pl.ds(c * size, size)]

    def slot(a, zz, yy, c):
        return piece(outs[a].at[zz * ny + yy], a, c)

    base = []
    total = 0
    for a in range(count):
        base.append(total)
        total += chunks[a]

    def own_copy(a):
        return pltpu.make_async_copy(ins[a], outs[a].at[me], own_sem.at[a])

    def level_z(lv):
        return z - lv if lv <= up else z + (lv - up)

    def source(lv, a, c):
        if lv == 0:
            return piece(ins[a], a, c)
        return slot(a, level_z(lv), y, c)

    def z_copy(lv, direction, a, c):
        there = (lv + 1) if direction > 0 else (up + 1 if lv == 0 else lv + 1)
        return pltpu.make_async_remote_copy(
            src_ref=source(lv, a, c),
            dst_ref=slot(a, level_z(lv), y, c),
            send_sem=zs_sem.at[there - 1, base[a] + c],
            recv_sem=zr_sem.at[there - 1, base[a] + c],
            device_id=dev(z + direction, y),
            device_id_type=MESH,
        )

    def z_cond(lv, direction):
        src = level_z(lv)
        return (src >= 0) & (src < nz) & (z + direction >= 0) & (z + direction < nz)

    def y_needed(lv, y_from, y_to):
        src = level_z(lv)
        ok = (src >= 0) & (src < nz)
        if window is not None:
            offset = (z - src) * ny + y_to - y_from
            ok = ok & (offset >= 0) & (offset <= window)
        return ok

    def y_copy(lv, dy, a, c):
        return pltpu.make_async_remote_copy(
            src_ref=source(lv, a, c),
            dst_ref=slot(a, level_z(lv), y, c),
            send_sem=ys_sem.at[lv * (ny - 1) + dy - 1, base[a] + c],
            recv_sem=yr_sem.at[lv * (ny - 1) + dy - 1, base[a] + c],
            device_id=dev(z, (y + dy) % ny),
            device_id_type=MESH,
        )

    def y_arrival(lv, dy, a, c):
        return pltpu.make_async_remote_copy(
            src_ref=source(lv, a, c),
            dst_ref=slot(a, level_z(lv), (y + ny - dy) % ny, c),
            send_sem=ys_sem.at[lv * (ny - 1) + dy - 1, base[a] + c],
            recv_sem=yr_sem.at[lv * (ny - 1) + dy - 1, base[a] + c],
            device_id=dev(z, (y + dy) % ny),
            device_id_type=MESH,
        )

    every = [(a, c) for a in range(count) for c in range(chunks[a])]

    def directions(lv):
        out = []
        if lv < up:
            out.append(1)
        if down and (lv == 0 or (lv > up and lv - up < down)):
            out.append(-1)
        return out

    def spread(lv, a, c):
        for direction in directions(lv):

            @pl.when(z_cond(lv, direction))
            def _(direction=direction):
                z_copy(lv, direction, a, c).start()

        for dy in range(1, ny):

            @pl.when(y_needed(lv, y, (y + dy) % ny))
            def _(dy=dy):
                y_copy(lv, dy, a, c).start()

    for a, c in every:
        spread(0, a, c)
    for a in range(count):
        own_copy(a).start()
    order = []
    for k in range(1, max(up, down) + 1):
        for a, c in every:
            if k <= up:
                order.append((k, a, c))
            if k <= down:
                order.append((up + k, a, c))
    for lv, a, c in order:
        src = level_z(lv)

        @pl.when((src >= 0) & (src < nz))
        def _(lv=lv, a=a, c=c):
            pltpu.make_async_remote_copy(
                src_ref=slot(a, level_z(lv), y, c),
                dst_ref=slot(a, level_z(lv), y, c),
                send_sem=zs_sem.at[lv - 1, base[a] + c],
                recv_sem=zr_sem.at[lv - 1, base[a] + c],
                device_id=dev(z, (y + 1) % ny),
                device_id_type=MESH,
            ).wait_recv()
            spread(lv, a, c)

    for lv in range(up + down + 1):
        for a, c in every:
            for dy in range(1, ny):

                @pl.when(y_needed(lv, (y + ny - dy) % ny, y))
                def _(lv=lv, a=a, c=c, dy=dy):
                    y_arrival(lv, dy, a, c).wait_recv()

    for lv in range(up + down + 1):
        for a, c in every:
            for direction in directions(lv):

                @pl.when(z_cond(lv, direction))
                def _(lv=lv, a=a, c=c, direction=direction):
                    z_copy(lv, direction, a, c).wait_send()

            for dy in range(1, ny):

                @pl.when(y_needed(lv, y, (y + dy) % ny))
                def _(lv=lv, a=a, c=c, dy=dy):
                    y_copy(lv, dy, a, c).wait_send()

    for a in range(count):
        own_copy(a).wait()


def seq_gather(arrays, ny, causal, chunks, collective_id):
    n = lax.axis_size("seq")
    nz = n // ny
    if causal:
        window = n // 2
        up, down = min(nz - 1, -(-window // ny)), 0
    else:
        window = None
        up = down = nz - 1
    count = len(arrays)
    total = sum(chunks)
    levels = up + down
    return pl.pallas_call(
        functools.partial(gather_kernel, nz, ny, up, down, window, chunks, count),
        out_shape=[jax.ShapeDtypeStruct((n,) + a.shape, a.dtype) for a in arrays],
        in_specs=[pl.BlockSpec(memory_space=VMEM)] * count,
        out_specs=[pl.BlockSpec(memory_space=pl.ANY)] * count,
        scratch_shapes=[
            pltpu.SemaphoreType.DMA((count,)),
            pltpu.SemaphoreType.DMA((levels, total)),
            pltpu.SemaphoreType.DMA((levels, total)),
            pltpu.SemaphoreType.DMA(((levels + 1) * (ny - 1), total)),
            pltpu.SemaphoreType.DMA(((levels + 1) * (ny - 1), total)),
        ],
        compiler_params=pltpu.CompilerParams(
            collective_id=collective_id, has_side_effects=True
        ),
    )(*arrays)


def attention_kernel(window, scale, q_ref, k_ref, v_ref, qdoc_ref, kdoc_ref, out_ref):
    here = lax.axis_index("seq")
    rows = q_ref.shape[0]
    query = q_ref[...]
    query_doc = qdoc_ref[...]
    row = lax.broadcasted_iota(jnp.int32, (rows, rows), 0)
    col = lax.broadcasted_iota(jnp.int32, (rows, rows), 1)
    first = jnp.maximum(here - window, 0)

    def visit(block, carry):
        top, total, accum = carry
        scores = (
            lax.dot_general(
                query,
                k_ref[block],
                (((1,), (1,)), ((), ())),
                preferred_element_type=jnp.float32,
            )
            * scale
        )
        visible = (query_doc == kdoc_ref[block, 0:1, :]) & (
            row - col >= (block - here) * rows
        )
        scores = jnp.where(visible, scores, masked_score)
        new_top = jnp.maximum(top, jnp.max(scores, axis=1, keepdims=True))
        weights = jnp.where(visible, jnp.exp(scores - new_top), 0.0)
        fade = jnp.exp(top - new_top)
        total = total * fade + jnp.sum(weights, axis=1, keepdims=True)
        accum = accum * fade + jnp.dot(
            weights.astype(jnp.bfloat16), v_ref[block], preferred_element_type=jnp.float32
        )
        return new_top, total, accum

    start = (
        jnp.full((rows, 1), masked_score, jnp.float32),
        jnp.zeros((rows, 1), jnp.float32),
        jnp.zeros((rows, HEAD_DIM), jnp.float32),
    )
    _, total, accum = lax.fori_loop(first, here + 1, visit, start)
    out_ref[...] = (accum / total).astype(jnp.bfloat16)


def attention(queries, keys, values, doc_col, doc_rows):
    rows, width = queries.shape
    n = keys.shape[0]
    heads = width // HEAD_DIM
    return pl.pallas_call(
        functools.partial(attention_kernel, n // 2, HEAD_DIM ** (-0.5)),
        grid=(heads,),
        out_shape=jax.ShapeDtypeStruct((rows, width), jnp.bfloat16),
        in_specs=[
            pl.BlockSpec((rows, HEAD_DIM), lambda h: (0, h)),
            pl.BlockSpec((n, rows, HEAD_DIM), lambda h: (0, 0, h)),
            pl.BlockSpec((n, rows, HEAD_DIM), lambda h: (0, 0, h)),
            pl.BlockSpec((rows, 1), lambda h: (0, 0)),
            pl.BlockSpec(doc_rows.shape, lambda h: (0, 0, 0)),
        ],
        out_specs=pl.BlockSpec((rows, HEAD_DIM), lambda h: (0, h)),
    )(queries, keys, values, doc_col, doc_rows)


def mp_scatter_kernel(n, x_ref, out_ref, near, sums, far, s1, r1, s2, r2):
    seq = lax.axis_index("seq")
    me = lax.axis_index("mp")
    chips = n // 2
    chip = me // 2
    core = me % 2
    partner = chip * 2 + 1 - core
    width = out_ref.shape[1]
    barrier = pltpu.get_barrier_semaphore()
    pl.semaphore_signal(barrier, inc=1, device_id=(seq, partner), device_id_type=MESH)
    for d in range(1, chips):
        other = ((chip + d) % chips) * 2 + core
        pl.semaphore_signal(barrier, inc=1, device_id=(seq, other), device_id_type=MESH)
    pl.semaphore_wait(barrier, chips)

    def columns(index):
        return pl.ds(pl.multiple_of(index * width, 128), width)

    first = []
    for d in list(range(1, chips)) + [0]:
        target = (chip + d) % chips
        copy = pltpu.make_async_remote_copy(
            src_ref=x_ref.at[:, columns(target * 2 + 1 - core)],
            dst_ref=near.at[d],
            send_sem=s1.at[d],
            recv_sem=r1.at[d],
            device_id=(seq, partner),
            device_id_type=MESH,
        )
        copy.start()
        first.append((d, target, copy))
    second = []
    for d, target, copy in first:
        copy.wait_recv()
        mine = x_ref[:, columns(target * 2 + core)].astype(jnp.float32)
        total = mine + near[d].astype(jnp.float32)
        if d == 0:
            out_ref[...] = total
            continue
        sums[d - 1] = total.astype(jnp.bfloat16)
        send = pltpu.make_async_remote_copy(
            src_ref=sums.at[d - 1],
            dst_ref=far.at[d - 1],
            send_sem=s2.at[d - 1],
            recv_sem=r2.at[d - 1],
            device_id=(seq, target * 2 + core),
            device_id_type=MESH,
        )
        send.start()
        second.append((d, send))
    for d, send in second:
        send.wait_recv()
        out_ref[...] += far[d - 1].astype(jnp.float32)
    for d, target, copy in first:
        copy.wait_send()
    for d, send in second:
        send.wait_send()


def mp_scatter(x, collective_id):
    n = lax.axis_size("mp")
    rows, total = x.shape
    width = total // n
    chips = n // 2
    return pl.pallas_call(
        functools.partial(mp_scatter_kernel, n),
        out_shape=jax.ShapeDtypeStruct((rows, width), jnp.float32),
        in_specs=[pl.BlockSpec(memory_space=VMEM)],
        out_specs=pl.BlockSpec(memory_space=VMEM),
        scratch_shapes=[
            VMEM((chips, rows, width), jnp.bfloat16),
            VMEM((chips - 1, rows, width), jnp.bfloat16),
            VMEM((chips - 1, rows, width), jnp.bfloat16),
            pltpu.SemaphoreType.DMA((chips,)),
            pltpu.SemaphoreType.DMA((chips,)),
            pltpu.SemaphoreType.DMA((chips - 1,)),
            pltpu.SemaphoreType.DMA((chips - 1,)),
        ],
        compiler_params=pltpu.CompilerParams(
            collective_id=collective_id, has_side_effects=True, vmem_limit_bytes=48 * 1024 * 1024
        ),
    )(x)


def seq_scatter_kernel(nz, ny, x_ref, out_ref, near, sums, far, s1, r1, s2, r2):
    me = lax.axis_index("seq")
    mp = lax.axis_index("mp")
    z = me // ny
    y = me % ny
    barrier = pltpu.get_barrier_semaphore()
    for d in range(1, ny):
        peer = z * ny + (y + d) % ny
        pl.semaphore_signal(barrier, inc=1, device_id=(peer, mp), device_id_type=MESH)
    for d in range(1, nz):
        peer = ((z + d) % nz) * ny + y
        pl.semaphore_signal(barrier, inc=1, device_id=(peer, mp), device_id_type=MESH)
    pl.semaphore_wait(barrier, ny + nz - 2)

    first = []
    for d in list(range(1, nz)) + [0]:
        target = (z + d) % nz
        group = []
        for e in range(1, ny):
            other = (y + e) % ny
            copy = pltpu.make_async_remote_copy(
                src_ref=x_ref.at[target * ny + other],
                dst_ref=near.at[d, e - 1],
                send_sem=s1.at[d, e - 1],
                recv_sem=r1.at[d, e - 1],
                device_id=(z * ny + other, mp),
                device_id_type=MESH,
            )
            copy.start()
            group.append(copy)
        first.append((d, target, group))
    second = []
    for d, target, group in first:
        total = x_ref[target * ny + y].astype(jnp.float32)
        for e, copy in enumerate(group):
            copy.wait_recv()
            total = total + near[d, e].astype(jnp.float32)
        if d == 0:
            out_ref[...] = total
            continue
        sums[d - 1] = total.astype(jnp.bfloat16)
        send = pltpu.make_async_remote_copy(
            src_ref=sums.at[d - 1],
            dst_ref=far.at[d - 1],
            send_sem=s2.at[d - 1],
            recv_sem=r2.at[d - 1],
            device_id=(target * ny + y, mp),
            device_id_type=MESH,
        )
        send.start()
        second.append((d, send))
    for d, send in second:
        send.wait_recv()
        out_ref[...] += far[d - 1].astype(jnp.float32)
    for d, target, group in first:
        for copy in group:
            copy.wait_send()
    for d, send in second:
        send.wait_send()


def seq_scatter(x, ny, collective_id):
    n, rows, width = x.shape
    nz = n // ny
    dma = pltpu.SemaphoreType.DMA
    return pl.pallas_call(
        functools.partial(seq_scatter_kernel, nz, ny),
        out_shape=jax.ShapeDtypeStruct((rows, width), jnp.float32),
        in_specs=[pl.BlockSpec(memory_space=VMEM)],
        out_specs=pl.BlockSpec(memory_space=VMEM),
        scratch_shapes=[
            VMEM((nz, ny - 1, rows, width), jnp.bfloat16),
            VMEM((nz - 1, rows, width), jnp.bfloat16),
            VMEM((nz - 1, rows, width), jnp.bfloat16),
            dma((nz, ny - 1)),
            dma((nz, ny - 1)),
            dma((nz - 1,)),
            dma((nz - 1,)),
        ],
        compiler_params=pltpu.CompilerParams(
            collective_id=collective_id, has_side_effects=True, vmem_limit_bytes=48 * 1024 * 1024
        ),
    )(x)


def reduce_pre(partial_pre, live):
    summed = lax.psum(partial_pre.astype(jnp.bfloat16), "mp").astype(jnp.float32)
    active = jnp.where(live[None, :], jnp.maximum(summed, 0.0), 0.0)
    column_sums = jnp.sum(active, axis=0)
    return (active.astype(jnp.bfloat16), column_sums)


def local(
    ny,
    resid,
    queries,
    keys,
    values,
    doc_ids,
    out_proj,
    ffn_gain,
    w_in,
    w_out,
    hot_index,
    hot_blocks,
):
    tok_dev, width_dev = resid.shape
    groups = lax.axis_size("seq")
    width = width_dev * lax.axis_size("mp")
    total_tokens = tok_dev * groups
    doc_row = jnp.broadcast_to(doc_ids[None, :], (8, tok_dev))
    doc_rows, all_keys, all_values = seq_gather(
        [doc_row, keys, values], ny, True, (1, 2, 2), 0
    )
    chosen = hot_index[0]
    slots = chosen.shape[0]
    hot_in = jnp.take(w_in, chosen, axis=1)
    hot_out = jnp.take(w_out, chosen, axis=0)
    live = jnp.arange(slots, dtype=jnp.int32) < BLOCK * hot_blocks[0]
    attended = attention(queries, all_keys, all_values, doc_ids[:, None], doc_rows)
    projected = jnp.dot(attended, out_proj, preferred_element_type=jnp.float32)
    projected = mp_scatter(projected.astype(jnp.bfloat16), 1)
    state_rows = (resid.astype(jnp.float32) + projected).astype(jnp.bfloat16)
    widened = state_rows.astype(jnp.float32)
    squares = lax.psum(jnp.sum(widened * widened, axis=1), "mp")
    inverse = lax.rsqrt(squares / width + epsilon)
    normed = (widened * inverse[:, None] * ffn_gain.astype(jnp.float32)).astype(jnp.bfloat16)
    (all_normed,) = seq_gather([normed], ny, False, (4,), 2)
    partial_pre = jnp.dot(
        all_normed.reshape(total_tokens, width_dev),
        hot_in,
        preferred_element_type=jnp.float32,
    )
    active_low, column_sums = reduce_pre(partial_pre, live)
    hot_mean = (column_sums / total_tokens)[None, :]
    contribution = jnp.dot(active_low, hot_out, preferred_element_type=jnp.float32)
    contribution = contribution.astype(jnp.bfloat16).reshape(groups, tok_dev, width_dev)
    ffn_out = seq_scatter(contribution, ny, 3)
    layer_out = (widened + ffn_out).astype(jnp.bfloat16)
    return (layer_out, hot_mean)


def solution(mesh):
    return jax.shard_map(
        functools.partial(local, row_length(mesh)),
        mesh=mesh,
        in_specs=(
            P("seq", "mp"),
            P("seq", "mp"),
            P("seq", "mp"),
            P("seq", "mp"),
            P("seq"),
            P("mp", None),
            P("mp"),
            P("mp", "seq"),
            P("seq", "mp"),
            P("seq", None),
            P("seq"),
        ),
        out_specs=(P("seq", "mp"), P("seq", None)),
        check_vma=False,
    )
```

profile of v0, /device:TPU:0, one launch (start us, length us, event | category | flops | bytes accessed | tf_op | source)
XLA Modules:
  0.0 354.1 jit_solution(15701410376798748848)
XLA Ops:
  7.2 0.0 all-reduce.2.cloned.1.call-start
  7.2 1.5 copy.13.qdoc_ref
  8.7 1.3 broadcast_in_dim.43.refs_0_
  10.0 33.0 %shard_map.122 = (s32[8,8,256]{2,1,0:T(8,128)}, bf16[8,256,1280]{2,1,0:T(8,128)(2,1)}, bf16[8,256,1280]{2,1,0:T(8,128)(2,1)}) custom-call(s32[8,256]{1,0:T(8,128)} %broadcast_in_dim.43.refs_0_, bf16[256,1280]{1,0:T(8,128)(2,1)} %refs_1_.1, bf16[256,1280]{1,0:T(8,128)(2,1)} %refs_2_.1), custom_call_target="tpu_custom_call" | custom-call | tf_op jit(solution)/shard_map/pallas_call | solution.py:217
  43.0 11.0 %shard_map.123 = bf16[256,1280]{1,0:T(8,128)(2,1)} custom-call(bf16[256,1280]{1,0:T(8,128)(2,1)} %q_ref.1, bf16[8,256,1280]{2,1,0:T(8,128)(2,1)} %get-tuple-element.5.k_ref, bf16[8,256,1280]{2,1,0:T(8,128)(2,1)} %get-tuple-element.6.v_ref, s32[256,1]{1,0:T(8,128)} %copy.13.qdoc_ref, s32[8,8,256]{2,1,0:T(8,128)} %get-tuple-element.7.kdoc_ref), custom_call_target="tpu_custom_call" | custom-call | tf_op jit(solution)/shard_map/pallas_call | solution.py:281
  54.0 8.5 %convolution_convert_fusion.1.x_ref = bf16[256,5120]{1,0:T(8,128)(2,1)S(1)} fusion(bf16[256,1280]{1,0:T(8,128)(2,1)} %shard_map.123, bf16[1280,5120]{1,0:T(8,128)(2,1)} %param.16), kind=kOutput, calls=%fused_computation.3 | convolution fusion | flops 3356753920 | bytes 16384000 | tf_op jit(solution)/shard_map/dot_general | solution.py:500
  62.5 0.0 copy-start.1
  62.5 0.0 copy-start.3
  62.5 19.4 %shard_map.124 = f32[256,1280]{1,0:T(8,128)S(1)} custom-call(bf16[256,5120]{1,0:T(8,128)(2,1)S(1)} %convolution_convert_fusion.1.x_ref), custom_call_target="tpu_custom_call" | custom-call | tf_op jit(solution)/shard_map/pallas_call | solution.py:360
  81.9 0.0 copy-done.1
  81.9 0.3 fusion.5
  82.2 5.8 %psum.14 = f32[256]{0:T(256)S(1)} all-reduce(f32[256]{0:T(256)S(1)} %get-tuple-element.8), channel_id=1, replica_groups=mesh['seq'=8,'mp'=4] {'mp'}, use_global_device_ids=true, to_apply=%region_1.2 | all-reduce | flops 256 | bytes 2048 | tf_op jit(solution)/shard_map/psum | solution.py:504
  88.0 0.0 copy-done.3
  88.0 1.1 fusion.7.refs_0_
  89.0 0.0 copy-start.2
  89.0 107.2 %shard_map.125 = bf16[8,256,1280]{2,1,0:T(8,128)(2,1)} custom-call(bf16[256,1280]{1,0:T(8,128)(2,1)} %fusion.7.refs_0_), custom_call_target="tpu_custom_call" | custom-call | tf_op jit(solution)/shard_map/pallas_call | solution.py:217
  196.3 0.0 copy-done.2
  196.4 6.0 %gather_fusion = bf16[384,1280]{1,0:T(8,128)(2,1)S(1)} fusion(bf16[1280,1728]{0,1:T(8,128)(2,1)} %param.18, s32[1024]{0:T(1024)S(1)} %pad_clamp_fusion), kind=kCustom, calls=%fused_computation | custom fusion | bytes 1967616 | tf_op jit(solution)/shard_map/jit(_take)/gather | solution.py:496
  202.4 6.6 %convolution_convert_fusion.2 = bf16[2048,384]{1,0:T(8,128)(2,1)} fusion(bf16[2048,1280]{1,0:T(8,128)(2,1)} %bitcast.9, bf16[384,1280]{1,0:T(8,128)(2,1)S(1)} %gather_fusion, pred[384]{0:T(512)(128)(4,1)S(1)} %compare_and_fusion), kind=kOutput, calls=%fused_computation.7 | convolution fusion | flops 2014543872 | bytes 7799168 | tf_op jit(solution)/shard_map/dot_general | solution.py:508
  209.0 0.0 all-reduce.2.cloned.1.call-update
  209.0 6.0 %gather_fusion.1 = bf16[384,1280]{1,0:T(8,128)(2,1)S(1)} fusion(bf16[1728,1280]{1,0:T(8,128)(2,1)} %param.19, s32[1024]{0:T(1024)S(1)} %pad_clamp_fusion), kind=kCustom, calls=%fused_computation.1 | custom fusion | bytes 1967616 | tf_op jit(solution)/shard_map/jit(_take)/gather | solution.py:497
  215.7 44.3 %all-reduce.2.cloned.1.call-done = bf16[2048,384]{1,0:T(8,128)(2,1)} async-done(((bf16[2048,384]{1,0:T(8,128)(2,1)}), bf16[2048,384]{1,0:T(8,128)(2,1)}) %all-reduce.2.cloned.1.call-update) | async-done | bytes 1572880 | tf_op jit(solution)/shard_map/psum | solution.py:466
  260.0 6.7 %convolution_convert_fusion = bf16[2048,1280]{1,0:T(8,128)(2,1)} fusion(bf16[2048,384]{1,0:T(8,128)(2,1)} %all-reduce.2.cloned.1.call-done, pred[384]{0:T(512)(128)(4,1)S(1)} %iota_compare_fusion, bf16[384,1280]{1,0:T(8,128)(2,1)S(1)} %gather_fusion.1, pred[384]{0:T(512)(128)(4,1)S(1)} %compare_and_fusion), kind=kOutput, calls=%fused_computation.2 | convolution fusion | flops 2019524608 | bytes 7799552 | tf_op jit(solution)/shard_map/dot_general | solution.py:515
  266.7 0.0 copy-start
  266.7 78.5 %shard_map.126 = f32[256,1280]{1,0:T(8,128)S(1)} custom-call(bf16[8,256,1280]{2,1,0:T(8,128)(2,1)} %bitcast.10), custom_call_target="tpu_custom_call" | custom-call | tf_op jit(solution)/shard_map/pallas_call | solution.py:445
  345.2 1.0 fusion.8
  346.2 0.0 copy-done
  346.2 0.5 fusion
  346.7 0.6 div.18
  (8 shorter events, 0.1 us)
Async XLA Ops:
  7.2 252.8 %all-reduce.2.cloned.1.call-start = ((), (), s32[]{:S(2)}) async-start(), calls=%async_computation | async-start | bytes 3145728 | tf_op jit(solution)/shard_map/psum | solution.py:466
  62.5 19.4 %copy-start.1 = (bf16[256,1280]{1,0:T(8,128)(2,1)S(1)}, bf16[256,1280]{1,0:T(8,128)(2,1)}, u32[]{:S(2)}) copy-start(bf16[256,1280]{1,0:T(8,128)(2,1)} %param.11) | copy-start | bytes 1966084
  62.5 25.4 %copy-start.3 = (bf16[1280]{0:T(1024)(128)(2,1)S(1)}, bf16[1280]{0:T(1024)(128)(2,1)}, u32[]{:S(2)}) copy-start(bf16[1280]{0:T(1024)(128)(2,1)} %param.17) | copy-start | bytes 7684
  89.0 107.2 %copy-start.2 = (s32[1,384]{1,0:T(1,128)S(1)}, s32[1,384]{1,0:T(1,128)}, u32[]{:S(2)}) copy-start(s32[1,384]{1,0:T(1,128)} %param.20) | copy-start | bytes 4612
  266.7 79.5 %copy-start = (bf16[2048,384]{1,0:T(8,128)(2,1)S(1)}, bf16[2048,384]{1,0:T(8,128)(2,1)}, u32[]{:S(2)}) copy-start(bf16[2048,384]{1,0:T(8,128)(2,1)} %all-reduce.2.cloned.1.call-done) | copy-start | bytes 4718596
Sparse Core Ops, SparseCore 0:
  209.2 50.7 all-reduce.1
where the time goes:
time: 355 us; the launch traced here: 354 us
  Pallas kernels  249 us (70%)
  waiting for transfers between devices  44.3 us (12%)
  matrix products  21.8 us (6%)
  local copies, waits for them, and re-layouts  15.4 us (4%)
  between operations  14.8 us (4%)
  blocking collectives  5.76 us (2%)
    pallas_call x2, Pallas kernels, seq_gather(): pl.pallas_call(functools.partial(gather_kernel, nz, ny, up, down, window,...  140 us
    pallas_call x1, Pallas kernels, seq_scatter(): pl.pallas_call(functools.partial(seq_scatter_kernel, nz, ny), out_shape=j...  78.5 us
    psum x1, waiting for transfers between devices, reduce_pre(): lax.psum(partial_pre.astype(jnp.bfloat16), 'mp').astype(jnp.float32)  44.3 us
    pallas_call x1, Pallas kernels, mp_scatter(): pl.pallas_call(functools.partial(mp_scatter_kernel, n), out_shape=jax.Sha...  19.4 us
    pallas_call x1, Pallas kernels, attention(): pl.pallas_call(functools.partial(attention_kernel, n // 2, HEAD_DIM ** (-...  11 us
    dot_general x1, matrix products, local(): projected = jnp.dot(attended, out_proj, preferred_element_type=jnp.float32)  8.5 us
  transfers between devices with their start and end apart: 1, of which 1 were waited for; matrix products, arithmetic and copies ran while one was open for 2% of the time, Pallas kernels for 0%

commit v1 on v0

--- a/solution.py
+++ b/solution.py
@@ -293,20 +293,27 @@
     )(queries, keys, values, doc_col, doc_rows)
 
 
-def mp_scatter_kernel(n, x_ref, out_ref, near, sums, far, s1, r1, s2, r2):
+def mp_scatter_kernel(n, ny, x_ref, w_ref, out_ref, all_ref, near, sums, far, s1, r1, s2, r2, ws, wr, own_sem):
     seq = lax.axis_index("seq")
     me = lax.axis_index("mp")
+    z = seq // ny
+    y = seq % ny
     chips = n // 2
     chip = me // 2
     core = me % 2
     partner = chip * 2 + 1 - core
     width = out_ref.shape[1]
+    slots = w_ref.shape[1]
     barrier = pltpu.get_barrier_semaphore()
     pl.semaphore_signal(barrier, inc=1, device_id=(seq, partner), device_id_type=MESH)
     for d in range(1, chips):
         other = ((chip + d) % chips) * 2 + core
         pl.semaphore_signal(barrier, inc=1, device_id=(seq, other), device_id_type=MESH)
-    pl.semaphore_wait(barrier, chips)
+    for d in range(1, ny):
+        pl.semaphore_signal(
+            barrier, inc=1, device_id=(z * ny + (y + d) % ny, me), device_id_type=MESH
+        )
+    pl.semaphore_wait(barrier, chips + ny - 1)
 
     def columns(index):
         return pl.ds(pl.multiple_of(index * width, 128), width)
@@ -324,6 +331,20 @@
         )
         copy.start()
         first.append((d, target, copy))
+    shared = []
+    for d in range(1, ny):
+        copy = pltpu.make_async_remote_copy(
+            src_ref=w_ref,
+            dst_ref=all_ref.at[:, pl.ds(d * slots, slots)],
+            send_sem=ws.at[d - 1],
+            recv_sem=wr.at[d - 1],
+            device_id=(z * ny + (y + ny - d) % ny, me),
+            device_id_type=MESH,
+        )
+        copy.start()
+        shared.append(copy)
+    own = pltpu.make_async_copy(w_ref, all_ref.at[:, pl.ds(0, slots)], own_sem)
+    own.start()
     second = []
     for d, target, copy in first:
         copy.wait_recv()
@@ -346,127 +367,399 @@
     for d, send in second:
         send.wait_recv()
         out_ref[...] += far[d - 1].astype(jnp.float32)
+    for copy in shared:
+        copy.wait_recv()
     for d, target, copy in first:
         copy.wait_send()
     for d, send in second:
         send.wait_send()
-
-
-def mp_scatter(x, collective_id):
+    for copy in shared:
+        copy.wait_send()
+    own.wait()
+
+
+def mp_scatter(x, hot_in, ny, collective_id):
     n = lax.axis_size("mp")
     rows, total = x.shape
     width = total // n
     chips = n // 2
+    depth, slots = hot_in.shape
+    dma = pltpu.SemaphoreType.DMA
     return pl.pallas_call(
-        functools.partial(mp_scatter_kernel, n),
-        out_shape=jax.ShapeDtypeStruct((rows, width), jnp.float32),
-        in_specs=[pl.BlockSpec(memory_space=VMEM)],
-        out_specs=pl.BlockSpec(memory_space=VMEM),
+        functools.partial(mp_scatter_kernel, n, ny),
+        out_shape=[
+            jax.ShapeDtypeStruct((rows, width), jnp.float32),
+            jax.ShapeDtypeStruct((depth, ny * slots), jnp.bfloat16),
+        ],
+        in_specs=[pl.BlockSpec(memory_space=VMEM)] * 2,
+        out_specs=[pl.BlockSpec(memory_space=VMEM), pl.BlockSpec(memory_space=pl.ANY)],
         scratch_shapes=[
             VMEM((chips, rows, width), jnp.bfloat16),
             VMEM((chips - 1, rows, width), jnp.bfloat16),
             VMEM((chips - 1, rows, width), jnp.bfloat16),
-            pltpu.SemaphoreType.DMA((chips,)),
-            pltpu.SemaphoreType.DMA((chips,)),
-            pltpu.SemaphoreType.DMA((chips - 1,)),
-            pltpu.SemaphoreType.DMA((chips - 1,)),
+            dma((chips,)),
+            dma((chips,)),
+            dma((chips - 1,)),
+            dma((chips - 1,)),
+            dma((ny - 1,)),
+            dma((ny - 1,)),
+            dma,
         ],
         compiler_params=pltpu.CompilerParams(
             collective_id=collective_id, has_side_effects=True, vmem_limit_bytes=48 * 1024 * 1024
         ),
-    )(x)
-
-
-def seq_scatter_kernel(nz, ny, x_ref, out_ref, near, sums, far, s1, r1, s2, r2):
-    me = lax.axis_index("seq")
-    mp = lax.axis_index("mp")
-    z = me // ny
-    y = me % ny
+    )(x, hot_in)
+
+
+def ffn_kernel(
+    nz, ny, nmp, count, total_tokens,
+    x_ref, state_ref, win_ref, wout_ref, out_ref, mean_ref,
+    win, wout, gathered, part, own_part, near, pair, active, contrib, moving, from_below, from_above,
+    hot, hot_near, hot_send, hot_other,
+    load_sem, ag_s, ag_r, pd_s, pd_r, px_s, px_r, ad_s, ad_r, up_s, up_r, dn_s, dn_r, wo_s, wo_r, hp_s, hp_r, hy_s, hy_r,
+):
+    f32 = jnp.float32
+    bf16 = jnp.bfloat16
+    seq = lax.axis_index("seq")
+    me = lax.axis_index("mp")
+    z = seq // ny
+    y = seq % ny
+    chips = nmp // 2
+    chip = me // 2
+    core = me % 2
+    rows, width = x_ref.shape
+    slots = wout_ref.shape[0]
+    size = rows // count
+    half = nz // 2
+    span = half * size
+    last = nz - 1
+    partner = (seq, chip * 2 + 1 - core)
+
+    def at_z(step):
+        return ((z + step) * ny + y, me)
+
+    def at_y(d):
+        return (z * ny + (y + d) % ny, me)
+
+    def at_x(d):
+        return (seq, ((chip + d) % chips) * 2 + core)
+
     barrier = pltpu.get_barrier_semaphore()
+
+    def greet(where):
+        pl.semaphore_signal(barrier, inc=1, device_id=where, device_id_type=MESH)
+
+    @pl.when(z > 0)
+    def _():
+        greet(at_z(-1))
+
+    @pl.when(z < last)
+    def _():
+        greet(at_z(1))
+
+    greet(partner)
+    for d in range(1, chips):
+        greet(at_x(d))
     for d in range(1, ny):
-        peer = z * ny + (y + d) % ny
-        pl.semaphore_signal(barrier, inc=1, device_id=(peer, mp), device_id_type=MESH)
-    for d in range(1, nz):
-        peer = ((z + d) % nz) * ny + y
-        pl.semaphore_signal(barrier, inc=1, device_id=(peer, mp), device_id_type=MESH)
-    pl.semaphore_wait(barrier, ny + nz - 2)
-
-    first = []
-    for d in list(range(1, nz)) + [0]:
-        target = (z + d) % nz
-        group = []
-        for e in range(1, ny):
-            other = (y + e) % ny
-            copy = pltpu.make_async_remote_copy(
-                src_ref=x_ref.at[target * ny + other],
-                dst_ref=near.at[d, e - 1],
-                send_sem=s1.at[d, e - 1],
-                recv_sem=r1.at[d, e - 1],
-                device_id=(z * ny + other, mp),
-                device_id_type=MESH,
-            )
-            copy.start()
-            group.append(copy)
-        first.append((d, target, group))
-    second = []
-    for d, target, group in first:
-        total = x_ref[target * ny + y].astype(jnp.float32)
-        for e, copy in enumerate(group):
-            copy.wait_recv()
-            total = total + near[d, e].astype(jnp.float32)
-        if d == 0:
-            out_ref[...] = total
-            continue
-        sums[d - 1] = total.astype(jnp.bfloat16)
-        send = pltpu.make_async_remote_copy(
-            src_ref=sums.at[d - 1],
-            dst_ref=far.at[d - 1],
-            send_sem=s2.at[d - 1],
-            recv_sem=r2.at[d - 1],
-            device_id=(target * ny + y, mp),
-            device_id_type=MESH,
-        )
-        send.start()
-        second.append((d, send))
-    for d, send in second:
-        send.wait_recv()
-        out_ref[...] += far[d - 1].astype(jnp.float32)
-    for d, target, group in first:
-        for copy in group:
-            copy.wait_send()
-    for d, send in second:
-        send.wait_send()
-
-
-def seq_scatter(x, ny, collective_id):
-    n, rows, width = x.shape
+        greet(at_y(d))
+    below = jnp.where(z > 0, 1, 0)
+    above = jnp.where(z < last, 1, 0)
+    pl.semaphore_wait(barrier, below + above + chips + ny - 1)
+
+    def remote(src, dst, send, recv, where):
+        return pltpu.make_async_remote_copy(
+            src_ref=src, dst_ref=dst, send_sem=send, recv_sem=recv,
+            device_id=where, device_id_type=MESH,
+        )
+
+    def own_rows(c):
+        return x_ref.at[pl.ds(c * size, size)]
+
+    def gather_copy(step, k, c):
+        block = z - step * k
+        src = own_rows(c) if k == 0 else gathered.at[c, block]
+        way = 0 if step > 0 else 1
+        return remote(src, gathered.at[c, block], ag_s.at[way, k, c], ag_r.at[block, c], at_z(step))
+
+    def can_pass(step, k):
+        block = z - step * k
+        there = z + step
+        return (block >= 0) & (block < nz) & (there >= 0) & (there < nz)
+
+    def pass_on(k, c, steps=(1, -1)):
+        for step in steps:
+
+            @pl.when(can_pass(step, k))
+            def _(step=step):
+                gather_copy(step, k, c).start()
+
+    def own_send(c):
+        pass_on(0, c)
+
+    def collect(c):
+        gathered[c, z] = x_ref[pl.ds(c * size, size), :]
+        for k in range(1, nz):
+            for step in (1, -1):
+                block = z - step * k
+
+                @pl.when((block >= 0) & (block < nz))
+                def _(step=step, k=k, block=block):
+                    remote(
+                        gathered.at[c, block], gathered.at[c, block],
+                        ag_s.at[0, 0, c], ag_r.at[block, c], partner,
+                    ).wait_recv()
+                    if k < nz - 1:
+                        pass_on(k, c, (step,))
+
+    def half_rows(side):
+        return pl.ds(side * half, half)
+
+    def pre_copy(c):
+        return remote(part.at[c], near.at[c], pd_s.at[c], pd_r.at[c], partner)
+
+    def multiply_in(c):
+        other = gathered[c, half_rows(1 - core)].reshape(span, width)
+        part[c] = jnp.dot(other, win[...], preferred_element_type=f32).astype(bf16)
+        pre_copy(c).start()
+        mine = gathered[c, half_rows(core)].reshape(span, width)
+        own_part[c] = jnp.dot(mine, win[...], preferred_element_type=f32)
+
+    def across_copy(d, c):
+        return remote(
+            pair.at[c, chip], pair.at[c, chip], px_s.at[d - 1, c], px_r.at[chip, c], at_x(d)
+        )
+
+    def exchange(c):
+        pre_copy(c).wait_recv()
+        pair[c, chip] = (own_part[c] + near[c].astype(f32)).astype(bf16)
+        for d in range(1, chips):
+            across_copy(d, c).start()
+
+    def active_copy(c):
+        return remote(
+            active.at[c, half_rows(core)], active.at[c, half_rows(core)],
+            ad_s.at[c], ad_r.at[c], partner,
+        )
+
+    def activate(c):
+        for d in range(1, chips):
+            other = (chip + d) % chips
+            remote(
+                pair.at[c, other], pair.at[c, other], px_s.at[d - 1, c], px_r.at[other, c], at_x(d)
+            ).wait_recv()
+        pre = pair[c, 0].astype(f32)
+        for k in range(1, chips):
+            pre = pre + pair[c, k].astype(f32)
+        value = jnp.maximum(pre, 0.0)
+        active[c, half_rows(core)] = value.astype(bf16).reshape(half, size, value.shape[1])
+        active_copy(c).start()
+        hot[...] += jnp.sum(value.reshape(span // 8, 8, value.shape[1]), axis=0)
+
+    def up_copy(t, c):
+        return remote(moving.at[c, t], from_below.at[c, t], up_s.at[t, c], up_r.at[t, c], at_z(1))
+
+    def down_copy(t, c):
+        return remote(moving.at[c, t], from_above.at[c, t], dn_s.at[t, c], dn_r.at[t, c], at_z(-1))
+
+    def multiply_out(c):
+        other = half_rows(1 - core)
+        remote(active.at[c, other], active.at[c, other], ad_s.at[c], ad_r.at[c], partner).wait_recv()
+        lhs = active[c].reshape(nz * size, active.shape[3])
+        contrib[c] = jnp.dot(lhs, wout[...], preferred_element_type=f32).reshape(nz, size, width)
+
+        @pl.when(z == 0)
+        def _():
+            for t in range(last, 0, -1):
+                moving[c, t] = contrib[c, t].astype(bf16)
+                up_copy(t, c).start()
+
+        @pl.when(z == last)
+        def _():
+            for t in range(last):
+                moving[c, t] = contrib[c, t].astype(bf16)
+                down_copy(t, c).start()
+
+    def middle(c):
+        for k in range(nz - 1, 0, -1):
+            up = z + k
+
+            @pl.when((z > 0) & (up < nz))
+            def _(up=up):
+                up_copy(up, c).wait_recv()
+                moving[c, up] = (contrib[c, up] + from_below[c, up].astype(f32)).astype(bf16)
+                up_copy(up, c).start()
+
+            down = z - k
+
+            @pl.when((z < last) & (down >= 0))
+            def _(down=down):
+                down_copy(down, c).wait_recv()
+                moving[c, down] = (contrib[c, down] + from_above[c, down].astype(f32)).astype(bf16)
+                down_copy(down, c).start()
+
+    def finish(c):
+        @pl.when(z > 0)
+        def _():
+            up_copy(z, c).wait_recv()
+            contrib[c, z] += from_below[c, z].astype(f32)
+
+        @pl.when(z < last)
+        def _():
+            down_copy(z, c).wait_recv()
+            contrib[c, z] += from_above[c, z].astype(f32)
+
+        here = pl.ds(c * size, size)
+        out_ref[here, :] = (state_ref[here, :].astype(f32) + contrib[c, z]).astype(bf16)
+
+    def wout_copy(d):
+        return remote(
+            wout_ref, wout.at[pl.ds(d * slots, slots)], wo_s.at[d - 1], wo_r.at[d - 1], at_y(ny - d)
+        )
+
+    own_send(0)
+    load_in = pltpu.make_async_copy(win_ref, win, load_sem.at[0])
+    load_in.start()
+    load_out = pltpu.make_async_copy(wout_ref, wout.at[pl.ds(0, slots)], load_sem.at[1])
+    load_out.start()
+    for d in range(1, ny):
+        wout_copy(d).start()
+    own_send(1)
+    hot[...] = jnp.zeros_like(hot)
+    for i in range(count + 2):
+        if i < count:
+            collect(i)
+            if i + 2 < count:
+                own_send(i + 2)
+            if i == 0:
+                load_in.wait()
+            multiply_in(i)
+        if 1 <= i <= count:
+            activate(i - 1)
+        if i < count:
+            exchange(i)
+        if i == 1:
+            load_out.wait()
+            for d in range(1, ny):
+                wout_copy(d).wait_recv()
+        if 1 <= i <= count:
+            multiply_out(i - 1)
+        if i >= 2:
+            middle(i - 2)
+
+    hot_pair = remote(hot, hot_near, hp_s, hp_r, partner)
+    hot_pair.start()
+    hot_pair.wait_recv()
+    both = jnp.sum(hot[...] + hot_near[...], axis=0, keepdims=True)
+    hot_send[...] = jnp.broadcast_to(both, hot_send.shape)
+
+    def mean_copy(d):
+        return remote(
+            hot_send.at[:, pl.ds(d * slots, slots)], hot_other.at[d - 1],
+            hy_s.at[d - 1], hy_r.at[d - 1], at_y(d),
+        )
+
+    for d in range(1, ny):
+        mean_copy(d).start()
+    for c in range(count):
+        finish(c)
+    total = hot_send[0:1, 0:slots]
+    for d in range(1, ny):
+        mean_copy(d).wait_recv()
+        total = total + hot_other[d - 1, 0:1, :]
+    mean_ref[...] = total / total_tokens
+
+    for c in range(count):
+        for k in range(nz - 1):
+            for step in (1, -1):
+
+                @pl.when(can_pass(step, k))
+                def _(step=step, k=k, c=c):
+                    gather_copy(step, k, c).wait_send()
+
+        pre_copy(c).wait_send()
+        for d in range(1, chips):
+            across_copy(d, c).wait_send()
+        active_copy(c).wait_send()
+        for t in range(nz):
+
+            @pl.when((t > z) & (z < last))
+            def _(t=t, c=c):
+                up_copy(t, c).wait_send()
+
+            @pl.when((t < z) & (z > 0))
+            def _(t=t, c=c):
+                down_copy(t, c).wait_send()
+
+    for d in range(1, ny):
+        wout_copy(d).wait_send()
+        mean_copy(d).wait_send()
+    hot_pair.wait_send()
+
+
+def ffn(normed, state, win, wout, ny, count, total_tokens, collective_id):
+    rows, width = normed.shape
+    slots = wout.shape[0]
+    n = lax.axis_size("seq")
+    nmp = lax.axis_size("mp")
     nz = n // ny
+    chips = nmp // 2
+    size = rows // count
+    span = (nz // 2) * size
+    wide = ny * slots
     dma = pltpu.SemaphoreType.DMA
+    vmem = pl.BlockSpec(memory_space=VMEM)
+    anywhere = pl.BlockSpec(memory_space=pl.ANY)
+    f32 = jnp.float32
+    bf16 = jnp.bfloat16
     return pl.pallas_call(
-        functools.partial(seq_scatter_kernel, nz, ny),
-        out_shape=jax.ShapeDtypeStruct((rows, width), jnp.float32),
-        in_specs=[pl.BlockSpec(memory_space=VMEM)],
-        out_specs=pl.BlockSpec(memory_space=VMEM),
+        functools.partial(ffn_kernel, nz, ny, nmp, count, total_tokens),
+        out_shape=[
+            jax.ShapeDtypeStruct((rows, width), bf16),
+            jax.ShapeDtypeStruct((1, slots), f32),
+        ],
+        in_specs=[vmem, vmem, anywhere, anywhere],
+        out_specs=[vmem, vmem],
         scratch_shapes=[
-            VMEM((nz, ny - 1, rows, width), jnp.bfloat16),
-            VMEM((nz - 1, rows, width), jnp.bfloat16),
-            VMEM((nz - 1, rows, width), jnp.bfloat16),
-            dma((nz, ny - 1)),
-            dma((nz, ny - 1)),
-            dma((nz - 1,)),
-            dma((nz - 1,)),
+            VMEM((width, wide), bf16),
+            VMEM((wide, width), bf16),
+            VMEM((count, nz, size, width), bf16),
+            VMEM((count, span, wide), bf16),
+            VMEM((count, span, wide), f32),
+            VMEM((count, span, wide), bf16),
+            VMEM((count, chips, span, wide), bf16),
+            VMEM((count, nz, size, wide), bf16),
+            VMEM((count, nz, size, width), f32),
+            VMEM((count, nz, size, width), bf16),
+            VMEM((count, nz, size, width), bf16),
+            VMEM((count, nz, size, width), bf16),
+            VMEM((8, wide), f32),
+            VMEM((8, wide), f32),
+            VMEM((8, wide), f32),
+            VMEM((ny - 1, 8, slots), f32),
+            dma((2,)),
+            dma((2, nz, count)),
+            dma((nz, count)),
+            dma((count,)),
+            dma((count,)),
+            dma((chips - 1, count)),
+            dma((chips, count)),
+            dma((count,)),
+            dma((count,)),
+            dma((nz, count)),
+            dma((nz, count)),
+            dma((nz, count)),
+            dma((nz, count)),
+            dma((ny - 1,)),
+            dma((ny - 1,)),
+            dma,
+            dma,
+            dma((ny - 1,)),
+            dma((ny - 1,)),
         ],
         compiler_params=pltpu.CompilerParams(
-            collective_id=collective_id, has_side_effects=True, vmem_limit_bytes=48 * 1024 * 1024
+            collective_id=collective_id, has_side_effects=True, vmem_limit_bytes=60 * 1024 * 1024
         ),
-    )(x)
-
-
-def reduce_pre(partial_pre, live):
-    summed = lax.psum(partial_pre.astype(jnp.bfloat16), "mp").astype(jnp.float32)
-    active = jnp.where(live[None, :], jnp.maximum(summed, 0.0), 0.0)
-    column_sums = jnp.sum(active, axis=0)
-    return (active.astype(jnp.bfloat16), column_sums)
+    )(normed, state, win, wout)
 
 
 def local(
@@ -493,30 +786,22 @@
     )
     chosen = hot_index[0]
     slots = chosen.shape[0]
-    hot_in = jnp.take(w_in, chosen, axis=1)
-    hot_out = jnp.take(w_out, chosen, axis=0)
     live = jnp.arange(slots, dtype=jnp.int32) < BLOCK * hot_blocks[0]
+    neurons = jnp.arange(w_in.shape[1], dtype=jnp.int32)
+    picks = ((neurons[:, None] == chosen[None, :]) & live[None, :]).astype(jnp.bfloat16)
+    hot_in = jnp.dot(w_in, picks, preferred_element_type=jnp.float32).astype(jnp.bfloat16)
+    hot_out = lax.dot_general(
+        picks, w_out, (((0,), (0,)), ((), ())), preferred_element_type=jnp.float32
+    ).astype(jnp.bfloat16)
     attended = attention(queries, all_keys, all_values, doc_ids[:, None], doc_rows)
     projected = jnp.dot(attended, out_proj, preferred_element_type=jnp.float32)
-    projected = mp_scatter(projected.astype(jnp.bfloat16), 1)
+    projected, win = mp_scatter(projected.astype(jnp.bfloat16), hot_in, ny, 1)
     state_rows = (resid.astype(jnp.float32) + projected).astype(jnp.bfloat16)
     widened = state_rows.astype(jnp.float32)
     squares = lax.psum(jnp.sum(widened * widened, axis=1), "mp")
     inverse = lax.rsqrt(squares / width + epsilon)
     normed = (widened * inverse[:, None] * ffn_gain.astype(jnp.float32)).astype(jnp.bfloat16)
-    (all_normed,) = seq_gather([normed], ny, False, (4,), 2)
-    partial_pre = jnp.dot(
-        all_normed.reshape(total_tokens, width_dev),
-        hot_in,
-        preferred_element_type=jnp.float32,
-    )
-    active_low, column_sums = reduce_pre(partial_pre, live)
-    hot_mean = (column_sums / total_tokens)[None, :]
-    contribution = jnp.dot(active_low, hot_out, preferred_element_type=jnp.float32)
-    contribution = contribution.astype(jnp.bfloat16).reshape(groups, tok_dev, width_dev)
-    ffn_out = seq_scatter(contribution, ny, 3)
-    layer_out = (widened + ffn_out).astype(jnp.bfloat16)
-    return (layer_out, hot_mean)
+    return ffn(normed, state_rows, win, hot_out, ny, 4, total_tokens, 2)
 
 
 def solution(mesh):

time: 355 us -> 252 us (0.71)
  waiting for transfers between devices: 44.3 us -> 0 us
  Pallas kernels: 249 us -> 215 us
  between operations: 14.8 us -> 1.36 us
  local copies, waits for them, and re-layouts: 15.4 us -> 7.24 us
    pallas_call x2 -> x1, Pallas kernels: 140 us -> 33 us  [seq_gather(): pl.pallas_call(functools.partial(gather_kernel, nz, ny, up, down, window,...]
    pallas_call x2, Pallas kernels: 97.9 us -> 171 us  [the longest x1 141 us: ffn(): pl.pallas_call(functools.partial(ffn_kernel, nz, ny, nmp, count, total_to...]
    psum x1 -> x0, waiting for transfers between devices: 44.3 us -> none  [reduce_pre(): lax.psum(partial_pre.astype(jnp.bfloat16), 'mp').astype(jnp.float32)]
    gather x2 -> x0, local copies, waits for them, and re-layouts: 12.1 us -> none  [the longest x1 6.03 us: local(): hot_out = jnp.take(w_out, chosen, axis=0)]
    unnamed x8 -> x12, local copies, waits for them, and re-layouts: 0.02 us -> 4.48 us
  transfers between devices with their start and end apart: 1 -> 0, of which waited for: 1 -> 0; matrix products, arithmetic and copies ran while one was open for 2% -> 0% of each run, Pallas kernels for 0% -> 0%
where the time goes in v1:
time: 252 us; the launch traced here: 251 us
  Pallas kernels  215 us (85%)
  matrix products  20.1 us (8%)
  local copies, waits for them, and re-layouts  7.24 us (3%)
  blocking collectives  6.15 us (2%)
    pallas_call x1, Pallas kernels, ffn(): pl.pallas_call(functools.partial(ffn_kernel, nz, ny, nmp, count, total_to...  141 us
    pallas_call x1, Pallas kernels, seq_gather(): pl.pallas_call(functools.partial(gather_kernel, nz, ny, up, down, window,...  33 us
    pallas_call x1, Pallas kernels, mp_scatter(): pl.pallas_call(functools.partial(mp_scatter_kernel, n, ny), out_shape=[ja...  29.7 us
    pallas_call x1, Pallas kernels, attention(): pl.pallas_call(functools.partial(attention_kernel, n // 2, HEAD_DIM ** (-...  11 us
    dot_general x1, matrix products, local(): projected = jnp.dot(attended, out_proj, preferred_element_type=jnp.float32)  10 us
    psum x1, blocking collectives, local(): squares = lax.psum(jnp.sum(widened * widened, axis=1), 'mp')  6.15 us
    dot_general x1, matrix products, local(): lax.dot_general(picks, w_out, (((0,), (0,)), ((), ())), preferred_element...  5.25 us

profile of v1, /device:TPU:0, one launch (start us, length us, event | category | flops | bytes accessed | tf_op | source)
XLA Modules:
  0.0 251.0 jit_solution(2033365224930140285)
XLA Ops:
  0.6 1.3 broadcast_in_dim.4.refs_0_
  1.9 33.0 %shard_map.122 = (s32[8,8,256]{2,1,0:T(8,128)}, bf16[8,256,1280]{2,1,0:T(8,128)(2,1)}, bf16[8,256,1280]{2,1,0:T(8,128)(2,1)}) custom-call(s32[8,256]{1,0:T(8,128)} %broadcast_in_dim.4.refs_0_, bf16[256,1280]{1,0:T(8,128)(2,1)} %refs_1_.1, bf16[256,1280]{1,0:T(8,128)(2,1)} %refs_2_.1), custom_call_target="tpu_custom_call" | custom-call | tf_op jit(solution)/shard_map/pallas_call | solution.py:217
  35.0 1.5 copy.14.qdoc_ref
  36.4 11.0 %shard_map.123 = bf16[256,1280]{1,0:T(8,128)(2,1)} custom-call(bf16[256,1280]{1,0:T(8,128)(2,1)} %q_ref.1, bf16[8,256,1280]{2,1,0:T(8,128)(2,1)} %get-tuple-element.7.k_ref, bf16[8,256,1280]{2,1,0:T(8,128)(2,1)} %get-tuple-element.8.v_ref, s32[256,1]{1,0:T(8,128)} %copy.14.qdoc_ref, s32[8,8,256]{2,1,0:T(8,128)} %get-tuple-element.9.kdoc_ref), custom_call_target="tpu_custom_call" | custom-call | tf_op jit(solution)/shard_map/pallas_call | solution.py:281
  47.4 0.0 copy-start.4
  47.4 10.0 %convolution_convert_fusion.x_ref = bf16[256,5120]{1,0:T(8,128)(2,1)} fusion(bf16[256,1280]{1,0:T(8,128)(2,1)} %shard_map.123, bf16[1280,5120]{1,0:T(8,128)(2,1)} %param.16), kind=kOutput, calls=%fused_computation | convolution fusion | flops 3356753920 | bytes 16384000 | tf_op jit(solution)/shard_map/dot_general | solution.py:797
  57.4 0.0 copy-done.4
  58.1 4.9 %fusion.3.w_ref = bf16[1280,384]{1,0:T(8,128)(2,1)S(1)} fusion(bf16[1280,1728]{0,1:T(8,128)(2,1)} %param.18, s32[384]{0:T(512)S(1)} %reduce, pred[384]{0:T(512)(128)(4,1)S(1)} %iota_compare_fusion.1), kind=kOutput, calls=%fused_computation.5 | convolution fusion | flops 1700511744 | bytes 5408640 | tf_op jit(solution)/shard_map/dot_general | solution.py:792
  63.0 0.0 copy-start.2
  63.0 0.0 copy-start.3
  63.0 29.7 %shard_map.124 = (f32[256,1280]{1,0:T(8,128)S(1)}, bf16[1280,768]{1,0:T(8,128)(2,1)S(1)}) custom-call(bf16[256,5120]{1,0:T(8,128)(2,1)} %convolution_convert_fusion.x_ref, bf16[1280,384]{1,0:T(8,128)(2,1)S(1)} %fusion.3.w_ref), custom_call_target="tpu_custom_call" | custom-call | tf_op jit(solution)/shard_map/pallas_call | solution.py:388
  92.7 0.0 copy-start
  92.7 1.3 copy-done
  94.0 0.0 copy-done.2
  94.0 0.3 fusion.10
  94.2 0.0 copy-start.1
  94.3 6.1 %psum.7 = f32[256]{0:T(256)S(1)} all-reduce(f32[256]{0:T(256)S(1)} %get-tuple-element.12), channel_id=1, replica_groups=mesh['seq'=8,'mp'=4] {'mp'}, use_global_device_ids=true, to_apply=%region_1.0 | all-reduce | flops 256 | bytes 2048 | tf_op jit(solution)/shard_map/psum | solution.py:801
  100.4 0.0 copy-done.3
  100.4 1.1 fusion.12.x_ref
  101.5 5.3 %convolution_convert_fusion.1.wout_ref = bf16[384,1280]{1,0:T(8,128)(2,1)} fusion(bf16[1728,1280]{1,0:T(8,128)(2,1)} %param.19, s32[384]{0:T(512)S(1)} %reduce, pred[384]{0:T(512)(128)(4,1)S(1)} %iota_compare_fusion.1), kind=kOutput, calls=%fused_computation.1 | convolution fusion | flops 1700511744 | bytes 5408640 | tf_op jit(solution)/shard_map/dot_general | solution.py:793
  106.7 0.0 copy-done.1
  106.7 141.1 %shard_map.125 = (bf16[256,1280]{1,0:T(8,128)(2,1)}, f32[1,384]{1,0:T(1,128)}) custom-call(bf16[256,1280]{1,0:T(8,128)(2,1)} %fusion.12.x_ref, bf16[256,1280]{1,0:T(8,128)(2,1)} %copy-done.1, bf16[1280,768]{1,0:T(8,128)(2,1)} %copy-done, bf16[384,1280]{1,0:T(8,128)(2,1)} %convolution_convert_fusion.1.wout_ref), custom_call_target="tpu_custom_call" | custom-call | tf_op jit(solution)/shard_map/pallas_call | solution.py:714
  247.8 2.0 copy.20
  249.8 1.2 copy.21
  (4 shorter events, 0.0 us)
Async XLA Ops:
  47.4 10.0 %copy-start.4 = (s32[1,384]{1,0:T(1,128)S(1)}, s32[1,384]{1,0:T(1,128)}, u32[]{:S(2)}) copy-start(s32[1,384]{1,0:T(1,128)} %param.20) | copy-start | bytes 4612
  63.0 31.0 %copy-start.2 = (bf16[256,1280]{1,0:T(8,128)(2,1)S(1)}, bf16[256,1280]{1,0:T(8,128)(2,1)}, u32[]{:S(2)}) copy-start(bf16[256,1280]{1,0:T(8,128)(2,1)} %param.11) | copy-start | bytes 1966084
  63.0 37.4 %copy-start.3 = (bf16[1280]{0:T(1024)(128)(2,1)S(1)}, bf16[1280]{0:T(1024)(128)(2,1)}, u32[]{:S(2)}) copy-start(bf16[1280]{0:T(1024)(128)(2,1)} %param.17) | copy-start | bytes 7684
  92.7 1.3 copy-start
  94.2 12.5 %copy-start.1 = (bf16[256,1280]{1,0:T(8,128)(2,1)}, bf16[256,1280]{1,0:T(8,128)(2,1)S(1)}, u32[]{:S(2)}) copy-start(bf16[256,1280]{1,0:T(8,128)(2,1)S(1)} %get-tuple-element.13.state_ref) | copy-start | bytes 1966084

commit v2 on v1

v2 whole, which is shorter than its diff:
```python
import functools

import jax
import jax.numpy as jnp
from jax import lax
from jax.experimental import pallas as pl
from jax.experimental.pallas import tpu as pltpu
from jax.sharding import PartitionSpec as P

HEAD_DIM = 128
BLOCK = 128
MESH = pl.DeviceIdType.MESH
VMEM = pltpu.VMEM

epsilon = 1e-05
masked_score = -1e30


def row_length(mesh):
    seq = mesh.shape["seq"]
    try:
        first = [mesh.devices[i, 0].coords for i in range(seq)]
        size = len({c[1] for c in first})
        if seq % size == 0:
            return size
    except (AttributeError, IndexError, TypeError):
        pass
    return 2


def front_kernel(
    nz, ny, nmp, up, window, per, scale,
    q_ref, k_ref, v_ref, doc_ref, qdoc_ref, resid_ref, gain_ref, row_ref, col_ref, win_hbm, wout_hbm, proj_hbm,
    state_ref, normed_ref, all_ref, hot_out_ref,
    kbuf, vbuf, docs, bias, scores, attended, proj, win, wout, hot_in,
    far_part, near_part, far_near, near_near, sums, far, total, squares,
    load_sem, z_s, y_s, recv, f_s, f_r, n_s, n_r, x_s, x_r, q_s, q_r, w_s, w_r, own_sem,
):
    f32 = jnp.float32
    bf16 = jnp.bfloat16
    seq = lax.axis_index("seq")
    me = lax.axis_index("mp")
    z = seq // ny
    y = seq % ny
    chips = nmp // 2
    chip = me // 2
    core = me % 2
    rows, width = q_ref.shape
    wide = per * HEAD_DIM
    count = width // wide
    slots = row_ref.shape[1]
    last = nz - 1
    partner = (seq, chip * 2 + 1 - core)

    barrier = pltpu.get_barrier_semaphore()

    def greet(where):
        pl.semaphore_signal(barrier, inc=1, device_id=where, device_id_type=MESH)

    above = ((z + 1) * ny + y, me)

    @pl.when(z > 0)
    def _():
        greet(((z - 1) * ny + y, me))

    @pl.when(z < last)
    def _():
        greet(above)

    for d in range(1, nmp):
        greet((seq, (me + d) % nmp))
    for d in range(1, ny):
        greet((z * ny + (y + d) % ny, me))
    has_below = jnp.where(z > 0, 1, 0)
    has_above = jnp.where(z < last, 1, 0)
    pl.semaphore_wait(barrier, has_below + has_above + nmp + ny - 2)

    def remote(src, dst, send, got, where):
        return pltpu.make_async_remote_copy(
            src_ref=src, dst_ref=dst, send_sem=send, recv_sem=got,
            device_id=where, device_id_type=MESH,
        )

    def cols(c):
        return pl.ds(pl.multiple_of(c * wide, 128), wide)

    def pieces(lv, c):
        slot = lv * ny - 1
        if lv == 0:
            return k_ref.at[:, cols(c)], v_ref.at[:, cols(c)]
        return kbuf.at[slot, :, cols(c)], vbuf.at[slot, :, cols(c)]

    def landing(o, c):
        return kbuf.at[o - 1, :, cols(c)], vbuf.at[o - 1, :, cols(c)]

    def copies(lv, o, c, send, where):
        if c is None:
            src = doc_ref if lv == 0 else docs.at[lv * ny]
            return [remote(src, docs.at[o], send.at[0], recv.at[o, 0], where)]
        out = []
        for j, (src, dst) in enumerate(zip(pieces(lv, c), landing(o, c))):
            p = 1 + 2 * c + j
            out.append(remote(src, dst, send.at[p], recv.at[o, p], where))
        return out

    def z_copies(lv, c):
        return copies(lv, (lv + 1) * ny, c, z_s.at[lv], above)

    def y_copies(lv, d, c):
        other = (y + d) % ny
        return copies(lv, lv * ny + other - y, c, y_s.at[lv, d - 1], (z * ny + other, me))

    def holds(lv):
        return z >= lv

    def y_wanted(lv, d):
        o = lv * ny + (y + d) % ny - y
        return holds(lv) & (o >= 0) & (o <= window)

    def spread(lv, c, act):
        if lv < up:

            @pl.when(holds(lv) & (z < last))
            def _():
                for copy in z_copies(lv, c):
                    act(copy)

        for d in range(1, ny):

            @pl.when(y_wanted(lv, d))
            def _(d=d):
                for copy in y_copies(lv, d, c):
                    act(copy)

    def start(copy):
        copy.start()

    def arrive(o, c):
        @pl.when(seq >= o)
        def _():
            if c is None:
                remote(docs.at[o], docs.at[o], z_s.at[0, 0], recv.at[o, 0], partner).wait_recv()
                return
            for j, dst in enumerate(landing(o, c)):
                p = 1 + 2 * c + j
                remote(dst, dst, z_s.at[0, p], recv.at[o, p], partner).wait_recv()

    spread(0, None, start)
    spread(0, 0, start)
    load_in = pltpu.make_async_copy(win_hbm, win, load_sem.at[0])
    load_in.start()
    load_out = pltpu.make_async_copy(wout_hbm, wout, load_sem.at[1])
    load_out.start()
    load_proj = pltpu.make_async_copy(proj_hbm, proj, load_sem.at[2])
    load_proj.start()
    for o in range(1, window + 1):

        @pl.when(seq < o)
        def _(o=o):
            kbuf[o - 1] = jnp.zeros((rows, width), bf16)
            vbuf[o - 1] = jnp.zeros((rows, width), bf16)
            docs[o] = jnp.full(docs.shape[1:], -1, jnp.int32)

    docs[0] = doc_ref[...]
    arrive(ny, None)
    spread(1, None, start)
    for c in range(1, count):
        spread(0, c, start)

    load_in.wait()
    hidden = win.shape[1]
    picks = (
        lax.broadcasted_iota(jnp.int32, (hidden, slots), 0) == row_ref[...]
    ).astype(f32).astype(bf16)
    step_in = 128

    @pl.loop(0, width // step_in)
    def _(r):
        here = pl.ds(pl.multiple_of(r * step_in, step_in), step_in)
        hot_in[here, :] = jnp.dot(win[here, :], picks, preferred_element_type=f32).astype(bf16)

    load_out.wait()

    @pl.loop(0, slots // BLOCK)
    def _(r):
        here = pl.ds(pl.multiple_of(r * BLOCK, BLOCK), BLOCK)
        chosen = (
            lax.broadcasted_iota(jnp.int32, (BLOCK, hidden), 1) == col_ref[here, :]
        ).astype(f32).astype(bf16)
        hot_out_ref[here, :] = jnp.dot(chosen, wout[...], preferred_element_type=f32).astype(bf16)

    for lv in range(1, up):

        @pl.loop(0, count)
        def _(c, lv=lv):
            arrive(lv * ny, c)
            spread(lv, c, start)

    for lv in range(2, up + 1):
        arrive(lv * ny, None)
        spread(lv, None, start)
    for o in range(1, window + 1):
        if o % ny:
            arrive(o, None)
    row = lax.broadcasted_iota(jnp.int32, (rows, rows), 0)
    col = lax.broadcasted_iota(jnp.int32, (rows, rows), 1)
    for o in range(window + 1):
        seen = qdoc_ref[...] == docs[o, 0:1, :]
        if o == 0:
            seen = seen & (row >= col)
        bias[o] = jnp.where(seen, 0.0, masked_score)

    factor = scale * 1.4426950408889634

    def attend(c):
        for o in range(1, window + 1):
            if o % ny:
                arrive(o, c)
        for h in range(per):
            here = pl.ds(pl.multiple_of(c * wide + h * HEAD_DIM, HEAD_DIM), HEAD_DIM)
            query = q_ref[:, here]
            top = None
            for o in range(window + 1):
                key = k_ref[:, here] if o == 0 else kbuf[o - 1, :, here]
                score = lax.dot_general(
                    query, key, (((1,), (1,)), ((), ())), preferred_element_type=f32
                ) + bias[o]
                scores[h, o] = score
                top = score if top is None else jnp.maximum(top, score)
            peak = jnp.max(top, axis=1, keepdims=True)
            accum = None
            for o in range(window + 1):
                value = v_ref[:, here] if o == 0 else vbuf[o - 1, :, here]
                both = jnp.concatenate([value, jnp.ones((rows, HEAD_DIM), bf16)], axis=1)
                weight = jnp.exp2((scores[h, o] - peak) * factor).astype(bf16)
                term = jnp.dot(weight, both, preferred_element_type=f32)
                accum = term if accum is None else accum + term
            attended[:, here] = (accum[:, :HEAD_DIM] / accum[:, HEAD_DIM:]).astype(bf16)

    @pl.loop(0, count + 1)
    def _(i):
        @pl.when(i < count)
        def _():
            arrive(up * ny, i)
            spread(up, i, start)

        @pl.when(i > 0)
        def _():
            attend(i - 1)

    shared = []
    for d in range(1, ny):
        copy = remote(
            hot_in, all_ref.at[:, pl.ds(d * slots, slots)], w_s.at[d - 1], w_r.at[d - 1],
            (z * ny + (y + ny - d) % ny, me),
        )
        copy.start()
        shared.append(copy)
    own = pltpu.make_async_copy(hot_in, all_ref.at[:, pl.ds(0, slots)], own_sem)
    own.start()
    load_proj.wait()

    parts = far_part.shape[1]
    band = rows // parts

    def block(r, target, side):
        where = pl.ds(pl.multiple_of((target * 2 + side) * width, 128), width)
        return jnp.dot(
            attended[pl.ds(r * band, band), :], proj[:, where], preferred_element_type=f32
        )

    far_copies = []
    for d in range(1, chips):
        for r in range(parts):
            far_part[d - 1, r] = block(r, (chip + d) % chips, 1 - core).astype(bf16)
            copy = remote(
                far_part.at[d - 1, r], far_near.at[d - 1, r], f_s.at[d - 1, r], f_r.at[d - 1, r],
                partner,
            )
            copy.start()
            far_copies.append(copy)
    across = []
    for d in range(1, chips):
        target = (chip + d) % chips
        for r in range(parts):
            mine = block(r, target, core)
            far_copies[(d - 1) * parts + r].wait_recv()
            sums[d - 1, r] = (mine + far_near[d - 1, r].astype(f32)).astype(bf16)
            copy = remote(
                sums.at[d - 1, r], far.at[d - 1, r], x_s.at[d - 1, r], x_r.at[d - 1, r],
                (seq, target * 2 + core),
            )
            copy.start()
            across.append(copy)
    near_copies = []
    for r in range(parts):
        near_part[r] = block(r, chip, 1 - core).astype(bf16)
        copy = remote(near_part.at[r], near_near.at[r], n_s.at[r], n_r.at[r], partner)
        copy.start()
        near_copies.append(copy)
    for r in range(parts):
        here = pl.ds(r * band, band)
        mine = block(r, chip, core)
        near_copies[r].wait_recv()
        total[here, :] = resid_ref[here, :].astype(f32) + (mine + near_near[r].astype(f32))
    lengths = []
    for r in range(parts):
        here = pl.ds(r * band, band)
        value = total[here, :]
        for d in range(1, chips):
            across[(d - 1) * parts + r].wait_recv()
            value = value + far[d - 1, r].astype(f32)
        state = value.astype(bf16)
        state_ref[here, :] = state
        widened = state.astype(f32)
        lengths.append(jnp.sum(widened * widened, axis=1, keepdims=True))
    length = jnp.concatenate(lengths, axis=0)
    flat = jnp.broadcast_to(length, (rows, 128)).T
    squares[me] = flat[0:8, :]
    for d in range(1, nmp):
        remote(
            squares.at[me], squares.at[me], q_s.at[d - 1], q_r.at[me], (seq, (me + d) % nmp)
        ).start()
    for d in range(1, nmp):
        other = (me + d) % nmp
        remote(
            squares.at[other], squares.at[other], q_s.at[d - 1], q_r.at[other], (seq, other)
        ).wait_recv()
    square = squares[0]
    for k in range(1, nmp):
        square = square + squares[k]
    inverse = lax.rsqrt(square / (width * nmp) + epsilon)
    column = jnp.broadcast_to(inverse[0:1, :], (128, rows)).T[:, 0:1]
    for r in range(parts):
        here = pl.ds(r * band, band)
        widened = state_ref[here, :].astype(f32)
        normed_ref[here, :] = (
            widened * column[r * band : (r + 1) * band] * gain_ref[...].astype(f32)
        ).astype(bf16)

    for lv in range(up + 1):
        spread(lv, None, lambda copy: copy.wait_send())

        @pl.loop(0, count)
        def _(c, lv=lv):
            spread(lv, c, lambda copy: copy.wait_send())

    for copy in far_copies + across + near_copies:
        copy.wait_send()
    for d in range(1, nmp):
        remote(
            squares.at[me], squares.at[me], q_s.at[d - 1], q_r.at[me], (seq, (me + d) % nmp)
        ).wait_send()
    for copy in shared:
        copy.wait()
    own.wait()


def front(queries, keys, values, doc_ids, resid, gain, chosen, w_in, w_out, out_proj, ny, collective_id):
    rows, width = queries.shape
    n = lax.axis_size("seq")
    nmp = lax.axis_size("mp")
    nz = n // ny
    chips = nmp // 2
    window = n // 2
    up = min(nz - 1, -(-window // ny))
    heads = width // HEAD_DIM
    per = 2 if heads % 2 == 0 else 1
    pieces = 1 + 2 * (heads // per)
    slots = chosen.shape[0]
    parts = 2
    band = rows // parts
    dma = pltpu.SemaphoreType.DMA
    vmem = pl.BlockSpec(memory_space=VMEM)
    anywhere = pl.BlockSpec(memory_space=pl.ANY)
    f32 = jnp.float32
    bf16 = jnp.bfloat16
    doc_row = jnp.broadcast_to(doc_ids[None, :], (8, rows))
    return pl.pallas_call(
        functools.partial(front_kernel, nz, ny, nmp, up, window, per, HEAD_DIM ** (-0.5)),
        out_shape=[
            jax.ShapeDtypeStruct((rows, width), bf16),
            jax.ShapeDtypeStruct((rows, width), bf16),
            jax.ShapeDtypeStruct((width, ny * slots), bf16),
            jax.ShapeDtypeStruct((slots, width), bf16),
        ],
        in_specs=[vmem] * 9 + [anywhere] * 3,
        out_specs=[vmem, vmem, anywhere, vmem],
        scratch_shapes=[
            VMEM((window, rows, width), bf16),
            VMEM((window, rows, width), bf16),
            VMEM((window + 1, 8, rows), jnp.int32),
            VMEM((window + 1, rows, rows), f32),
            VMEM((per, window + 1, rows, rows), f32),
            VMEM((rows, width), bf16),
            VMEM(out_proj.shape, bf16),
            VMEM(w_in.shape, bf16),
            VMEM(w_out.shape, bf16),
            VMEM((width, slots), bf16),
            VMEM((chips - 1, parts, band, width), bf16),
            VMEM((parts, band, width), bf16),
            VMEM((chips - 1, parts, band, width), bf16),
            VMEM((parts, band, width), bf16),
            VMEM((chips - 1, parts, band, width), bf16),
            VMEM((chips - 1, parts, band, width), bf16),
            VMEM((rows, width), f32),
            VMEM((nmp, 8, rows), f32),
            dma((3,)),
            dma((up, pieces)),
            dma((up + 1, ny - 1, pieces)),
            dma((window + 1, pieces)),
            dma((chips - 1, parts)),
            dma((chips - 1, parts)),
            dma((parts,)),
            dma((parts,)),
            dma((chips - 1, parts)),
            dma((chips - 1, parts)),
            dma((nmp - 1,)),
            dma((nmp,)),
            dma((ny - 1,)),
            dma((ny - 1,)),
            dma,
        ],
        compiler_params=pltpu.CompilerParams(
            collective_id=collective_id, has_side_effects=True, vmem_limit_bytes=63 * 1024 * 1024
        ),
    )(
        queries, keys, values, doc_row, doc_ids[:, None], resid, gain[None, :],
        chosen[None, :], chosen[:, None], w_in, w_out, out_proj,
    )


def ffn_kernel(
    nz, ny, nmp, count, total_tokens,
    x_ref, state_ref, win_ref, wout_ref, out_ref, mean_ref,
    win, wout, gathered, part, own_part, near, pair, active, contrib, moving, from_below, from_above,
    hot, hot_near, hot_send, hot_other,
    load_sem, ag_s, ag_r, pd_s, pd_r, px_s, px_r, ad_s, ad_r, up_s, up_r, dn_s, dn_r, wo_s, wo_r, hp_s, hp_r, hy_s, hy_r,
):
    f32 = jnp.float32
    bf16 = jnp.bfloat16
    seq = lax.axis_index("seq")
    me = lax.axis_index("mp")
    z = seq // ny
    y = seq % ny
    chips = nmp // 2
    chip = me // 2
    core = me % 2
    rows, width = x_ref.shape
    slots = wout_ref.shape[0]
    size = rows // count
    half = nz // 2
    span = half * size
    last = nz - 1
    partner = (seq, chip * 2 + 1 - core)

    def at_z(step):
        return ((z + step) * ny + y, me)

    def at_y(d):
        return (z * ny + (y + d) % ny, me)

    def at_x(d):
        return (seq, ((chip + d) % chips) * 2 + core)

    barrier = pltpu.get_barrier_semaphore()

    def greet(where):
        pl.semaphore_signal(barrier, inc=1, device_id=where, device_id_type=MESH)

    @pl.when(z > 0)
    def _():
        greet(at_z(-1))

    @pl.when(z < last)
    def _():
        greet(at_z(1))

    greet(partner)
    for d in range(1, chips):
        greet(at_x(d))
    for d in range(1, ny):
        greet(at_y(d))
    below = jnp.where(z > 0, 1, 0)
    above = jnp.where(z < last, 1, 0)
    pl.semaphore_wait(barrier, below + above + chips + ny - 1)

    def remote(src, dst, send, recv, where):
        return pltpu.make_async_remote_copy(
            src_ref=src, dst_ref=dst, send_sem=send, recv_sem=recv,
            device_id=where, device_id_type=MESH,
        )

    def own_rows(c):
        return x_ref.at[pl.ds(c * size, size)]

    def gather_copy(step, k, c):
        block = z - step * k
        src = own_rows(c) if k == 0 else gathered.at[c, block]
        way = 0 if step > 0 else 1
        return remote(src, gathered.at[c, block], ag_s.at[way, k, c], ag_r.at[block, c], at_z(step))

    def can_pass(step, k):
        block = z - step * k
        there = z + step
        return (block >= 0) & (block < nz) & (there >= 0) & (there < nz)

    def pass_on(k, c, steps=(1, -1)):
        for step in steps:

            @pl.when(can_pass(step, k))
            def _(step=step):
                gather_copy(step, k, c).start()

    def own_send(c):
        pass_on(0, c)

    def collect(c):
        gathered[c, z] = x_ref[pl.ds(c * size, size), :]
        for k in range(1, nz):
            for step in (1, -1):
                block = z - step * k

                @pl.when((block >= 0) & (block < nz))
                def _(step=step, k=k, block=block):
                    remote(
                        gathered.at[c, block], gathered.at[c, block],
                        ag_s.at[0, 0, c], ag_r.at[block, c], partner,
                    ).wait_recv()
                    if k < nz - 1:
                        pass_on(k, c, (step,))

    def half_rows(side):
        return pl.ds(side * half, half)

    def pre_copy(c):
        return remote(part.at[c], near.at[c], pd_s.at[c], pd_r.at[c], partner)

    def multiply_in(c):
        other = gathered[c, half_rows(1 - core)].reshape(span, width)
        part[c] = jnp.dot(other, win[...], preferred_element_type=f32).astype(bf16)
        pre_copy(c).start()
        mine = gathered[c, half_rows(core)].reshape(span, width)
        own_part[c] = jnp.dot(mine, win[...], preferred_element_type=f32)

    def across_copy(d, c):
        return remote(
            pair.at[c, chip], pair.at[c, chip], px_s.at[d - 1, c], px_r.at[chip, c], at_x(d)
        )

    def exchange(c):
        pre_copy(c).wait_recv()
        pair[c, chip] = (own_part[c] + near[c].astype(f32)).astype(bf16)
        for d in range(1, chips):
            across_copy(d, c).start()

    def active_copy(c):
        return remote(
            active.at[c, half_rows(core)], active.at[c, half_rows(core)],
            ad_s.at[c], ad_r.at[c], partner,
        )

    def activate(c):
        for d in range(1, chips):
            other = (chip + d) % chips
            remote(
                pair.at[c, other], pair.at[c, other], px_s.at[d - 1, c], px_r.at[other, c], at_x(d)
            ).wait_recv()
        pre = pair[c, 0].astype(f32)
        for k in range(1, chips):
            pre = pre + pair[c, k].astype(f32)
        value = jnp.maximum(pre, 0.0)
        active[c, half_rows(core)] = value.astype(bf16).reshape(half, size, value.shape[1])
        active_copy(c).start()
        hot[...] += jnp.sum(value.reshape(span // 8, 8, value.shape[1]), axis=0)

    def up_copy(t, c):
        return remote(moving.at[c, t], from_below.at[c, t], up_s.at[t, c], up_r.at[t, c], at_z(1))

    def down_copy(t, c):
        return remote(moving.at[c, t], from_above.at[c, t], dn_s.at[t, c], dn_r.at[t, c], at_z(-1))

    def multiply_out(c):
        other = half_rows(1 - core)
        remote(active.at[c, other], active.at[c, other], ad_s.at[c], ad_r.at[c], partner).wait_recv()
        lhs = active[c].reshape(nz * size, active.shape[3])
        contrib[c] = jnp.dot(lhs, wout[...], preferred_element_type=f32).reshape(nz, size, width)

        @pl.when(z == 0)
        def _():
            for t in range(last, 0, -1):
                moving[c, t] = contrib[c, t].astype(bf16)
                up_copy(t, c).start()

        @pl.when(z == last)
        def _():
            for t in range(last):
                moving[c, t] = contrib[c, t].astype(bf16)
                down_copy(t, c).start()

    def middle(c):
        for k in range(nz - 1, 0, -1):
            up = z + k

            @pl.when((z > 0) & (up < nz))
            def _(up=up):
                up_copy(up, c).wait_recv()
                moving[c, up] = (contrib[c, up] + from_below[c, up].astype(f32)).astype(bf16)
                up_copy(up, c).start()

            down = z - k

            @pl.when((z < last) & (down >= 0))
            def _(down=down):
                down_copy(down, c).wait_recv()
                moving[c, down] = (contrib[c, down] + from_above[c, down].astype(f32)).astype(bf16)
                down_copy(down, c).start()

    def finish(c):
        @pl.when(z > 0)
        def _():
            up_copy(z, c).wait_recv()
            contrib[c, z] += from_below[c, z].astype(f32)

        @pl.when(z < last)
        def _():
            down_copy(z, c).wait_recv()
            contrib[c, z] += from_above[c, z].astype(f32)

        here = pl.ds(c * size, size)
        out_ref[here, :] = (state_ref[here, :].astype(f32) + contrib[c, z]).astype(bf16)

    def wout_copy(d):
        return remote(
            wout_ref, wout.at[pl.ds(d * slots, slots)], wo_s.at[d - 1], wo_r.at[d - 1], at_y(ny - d)
        )

    own_send(0)
    load_in = pltpu.make_async_copy(win_ref, win, load_sem.at[0])
    load_in.start()
    load_out = pltpu.make_async_copy(wout_ref, wout.at[pl.ds(0, slots)], load_sem.at[1])
    load_out.start()
    for d in range(1, ny):
        wout_copy(d).start()
    own_send(1)
    hot[...] = jnp.zeros_like(hot)
    for i in range(count + 2):
        if i < count:
            collect(i)
            if i + 2 < count:
                own_send(i + 2)
            if i == 0:
                load_in.wait()
            multiply_in(i)
        if 1 <= i <= count:
            activate(i - 1)
        if i < count:
            exchange(i)
        if i == 1:
            load_out.wait()
            for d in range(1, ny):
                wout_copy(d).wait_recv()
        if 1 <= i <= count:
            multiply_out(i - 1)
        if i >= 2:
            middle(i - 2)

    hot_pair = remote(hot, hot_near, hp_s, hp_r, partner)
    hot_pair.start()
    hot_pair.wait_recv()
    both = jnp.sum(hot[...] + hot_near[...], axis=0, keepdims=True)
    hot_send[...] = jnp.broadcast_to(both, hot_send.shape)

    def mean_copy(d):
        return remote(
            hot_send.at[:, pl.ds(d * slots, slots)], hot_other.at[d - 1],
            hy_s.at[d - 1], hy_r.at[d - 1], at_y(d),
        )

    for d in range(1, ny):
        mean_copy(d).start()
    for c in range(count):
        finish(c)
    total = hot_send[0:1, 0:slots]
    for d in range(1, ny):
        mean_copy(d).wait_recv()
        total = total + hot_other[d - 1, 0:1, :]
    mean_ref[...] = total / total_tokens

    for c in range(count):
        for k in range(nz - 1):
            for step in (1, -1):

                @pl.when(can_pass(step, k))
                def _(step=step, k=k, c=c):
                    gather_copy(step, k, c).wait_send()

        pre_copy(c).wait_send()
        for d in range(1, chips):
            across_copy(d, c).wait_send()
        active_copy(c).wait_send()
        for t in range(nz):

            @pl.when((t > z) & (z < last))
            def _(t=t, c=c):
                up_copy(t, c).wait_send()

            @pl.when((t < z) & (z > 0))
            def _(t=t, c=c):
                down_copy(t, c).wait_send()

    for d in range(1, ny):
        wout_copy(d).wait_send()
        mean_copy(d).wait_send()
    hot_pair.wait_send()


def ffn(normed, state, win, wout, ny, count, total_tokens, collective_id):
    rows, width = normed.shape
    slots = wout.shape[0]
    n = lax.axis_size("seq")
    nmp = lax.axis_size("mp")
    nz = n // ny
    chips = nmp // 2
    size = rows // count
    span = (nz // 2) * size
    wide = ny * slots
    dma = pltpu.SemaphoreType.DMA
    vmem = pl.BlockSpec(memory_space=VMEM)
    anywhere = pl.BlockSpec(memory_space=pl.ANY)
    f32 = jnp.float32
    bf16 = jnp.bfloat16
    return pl.pallas_call(
        functools.partial(ffn_kernel, nz, ny, nmp, count, total_tokens),
        out_shape=[
            jax.ShapeDtypeStruct((rows, width), bf16),
            jax.ShapeDtypeStruct((1, slots), f32),
        ],
        in_specs=[vmem, vmem, anywhere, anywhere],
        out_specs=[vmem, vmem],
        scratch_shapes=[
            VMEM((width, wide), bf16),
            VMEM((wide, width), bf16),
            VMEM((count, nz, size, width), bf16),
            VMEM((count, span, wide), bf16),
            VMEM((count, span, wide), f32),
            VMEM((count, span, wide), bf16),
            VMEM((count, chips, span, wide), bf16),
            VMEM((count, nz, size, wide), bf16),
            VMEM((count, nz, size, width), f32),
            VMEM((count, nz, size, width), bf16),
            VMEM((count, nz, size, width), bf16),
            VMEM((count, nz, size, width), bf16),
            VMEM((8, wide), f32),
            VMEM((8, wide), f32),
            VMEM((8, wide), f32),
            VMEM((ny - 1, 8, slots), f32),
            dma((2,)),
            dma((2, nz, count)),
            dma((nz, count)),
            dma((count,)),
            dma((count,)),
            dma((chips - 1, count)),
            dma((chips, count)),
            dma((count,)),
            dma((count,)),
            dma((nz, count)),
            dma((nz, count)),
            dma((nz, count)),
            dma((nz, count)),
            dma((ny - 1,)),
            dma((ny - 1,)),
            dma,
            dma,
            dma((ny - 1,)),
            dma((ny - 1,)),
        ],
        compiler_params=pltpu.CompilerParams(
            collective_id=collective_id, has_side_effects=True, vmem_limit_bytes=60 * 1024 * 1024
        ),
    )(normed, state, win, wout)


def local(
    ny,
    resid,
    queries,
    keys,
    values,
    doc_ids,
    out_proj,
    ffn_gain,
    w_in,
    w_out,
    hot_index,
    hot_blocks,
):
    rows = resid.shape[0]
    total_tokens = rows * lax.axis_size("seq")
    slots = hot_index.shape[1]
    live = jnp.arange(slots, dtype=jnp.int32) < BLOCK * hot_blocks[0]
    chosen = jnp.where(live, hot_index[0], -1)
    state, normed, win, hot_out = front(
        queries, keys, values, doc_ids, resid, ffn_gain, chosen, w_in, w_out, out_proj, ny, 0
    )
    return ffn(normed, state, win, hot_out, ny, 4, total_tokens, 1)


def solution(mesh):
    return jax.shard_map(
        functools.partial(local, row_length(mesh)),
        mesh=mesh,
        in_specs=(
            P("seq", "mp"),
            P("seq", "mp"),
            P("seq", "mp"),
            P("seq", "mp"),
            P("seq"),
            P("mp", None),
            P("mp"),
            P("mp", "seq"),
            P("seq", "mp"),
            P("seq", None),
            P("seq"),
        ),
        out_specs=(P("seq", "mp"), P("seq", None)),
        check_vma=False,
    )
```

time: 252 us -> 210 us (0.83)
  Pallas kernels: 215 us -> 191 us
  matrix products: 20.1 us -> 0 us
  local copies, waits for them, and re-layouts: 7.24 us -> 15.2 us
  blocking collectives: 6.15 us -> 0 us
    dot_general x3 -> x0, matrix products: 20.1 us -> none  [the longest x1 10 us: local(): projected = jnp.dot(attended, out_proj, preferred_element_type=jnp.float32)]
    pallas_call x3 -> x1, Pallas kernels: 73.7 us -> 61.5 us  [front(): pl.pallas_call(functools.partial(front_kernel, nz, ny, nmp, up, window, p...]
    pallas_call x1, Pallas kernels: 141 us -> 130 us  [ffn(): pl.pallas_call(functools.partial(ffn_kernel, nz, ny, nmp, count, total_to...]
    psum x1 -> x0, blocking collectives: 6.15 us -> none  [local(): squares = lax.psum(jnp.sum(widened * widened, axis=1), 'mp')]
    unnamed x12 -> x3, local copies, waits for them, and re-layouts: 4.48 us -> 10.3 us
where the time goes in v2:
time: 210 us
  Pallas kernels  191 us (91%)
  local copies, waits for them, and re-layouts  15.2 us (7%)
    pallas_call x1, Pallas kernels, ffn(): pl.pallas_call(functools.partial(ffn_kernel, nz, ny, nmp, count, total_to...  130 us
    pallas_call x1, Pallas kernels, front(): pl.pallas_call(functools.partial(front_kernel, nz, ny, nmp, up, window, p...  61.5 us
    unnamed x3, local copies, waits for them, and re-layouts  10.3 us

profile of v2, /device:TPU:0, one launch (start us, length us, event | category | flops | bytes accessed | tf_op | source)
XLA Modules:
  0.0 209.7 jit_solution(17364523537899615486)
XLA Ops:
  1.3 1.2 compare_select_fusion.row_ref
  2.5 1.3 broadcast_in_dim.22.gain_ref
  3.8 1.3 broadcast_in_dim.20.doc_ref
  5.1 1.5 copy.15.qdoc_ref
  6.6 0.8 copy.14
  7.4 0.7 fusion.col_ref
  8.1 7.2 %copy.16.win_hbm = bf16[1280,1728]{1,0:T(8,128)(2,1)} copy(bf16[1280,1728]{0,1:T(8,128)(2,1)} %param.18) | data formatting | bytes 8847360 | tf_op args[7]
  15.3 61.5 %shard_map.122 = (bf16[256,1280]{1,0:T(8,128)(2,1)}, bf16[256,1280]{1,0:T(8,128)(2,1)}, bf16[1280,768]{1,0:T(8,128)(2,1)}, bf16[384,1280]{1,0:T(8,128)(2,1)}) custom-call(bf16[256,1280]{1,0:T(8,128)(2,1)} %q_ref.1, bf16[256,1280]{1,0:T(8,128)(2,1)} %k_ref.1, bf16[256,1280]{1,0:T(8,128)(2,1)} %v_ref.1, s32[8,256]{1,0:T(8,128)} %broadcast_in_dim.20.doc_ref, ...), custom_call_target="tpu_custom_call" | custom-call | tf_op jit(solution)/shard_map/pallas_call | solution.py:379
  76.8 129.7 %shard_map.123 = (bf16[256,1280]{1,0:T(8,128)(2,1)}, f32[1,384]{1,0:T(1,128)}) custom-call(bf16[256,1280]{1,0:T(8,128)(2,1)} %get-tuple-element.6.x_ref, bf16[256,1280]{1,0:T(8,128)(2,1)} %get-tuple-element.7.state_ref, bf16[1280,768]{1,0:T(8,128)(2,1)} %get-tuple-element.8.win_ref, bf16[384,1280]{1,0:T(8,128)(2,1)} %get-tuple-element.9.wout_ref), custom_call_target="tpu_custom_call" | custom-call | tf_op jit(solution)/shard_map/pallas_call | solution.py:733
  206.6 2.0 copy.20
  208.5 1.2 copy.21

commit v3 on v2

--- a/solution.py
+++ b/solution.py
@@ -30,7 +30,7 @@
 
 def front_kernel(
     nz, ny, nmp, up, window, per, scale,
-    q_ref, k_ref, v_ref, doc_ref, qdoc_ref, resid_ref, gain_ref, row_ref, col_ref, win_hbm, wout_hbm, proj_hbm,
+    q_ref, k_ref, v_ref, doc_ref, resid_ref, gain_ref, index_ref, live_ref, win_hbm, wout_hbm, proj_hbm,
     state_ref, normed_ref, all_ref, hot_out_ref,
     kbuf, vbuf, docs, bias, scores, attended, proj, win, wout, hot_in,
     far_part, near_part, far_near, near_near, sums, far, total, squares,
@@ -48,7 +48,7 @@
     rows, width = q_ref.shape
     wide = per * HEAD_DIM
     count = width // wide
-    slots = row_ref.shape[1]
+    slots = index_ref.shape[1]
     last = nz - 1
     partner = (seq, chip * 2 + 1 - core)
 
@@ -168,26 +168,22 @@
         spread(0, c, start)
 
     load_in.wait()
-    hidden = win.shape[1]
-    picks = (
-        lax.broadcasted_iota(jnp.int32, (hidden, slots), 0) == row_ref[...]
-    ).astype(f32).astype(bf16)
-    step_in = 128
-
-    @pl.loop(0, width // step_in)
-    def _(r):
-        here = pl.ds(pl.multiple_of(r * step_in, step_in), step_in)
-        hot_in[here, :] = jnp.dot(win[here, :], picks, preferred_element_type=f32).astype(bf16)
-
+    hidden = win.shape[0]
+    order = lax.broadcasted_iota(jnp.int32, (1, slots), 1)
+    chosen = jnp.where(order < BLOCK * live_ref[0], index_ref[...], -1).astype(f32)
+    chosen = jnp.broadcast_to(chosen, (BLOCK, slots))
+    neurons = lax.broadcasted_iota(jnp.int32, (BLOCK, hidden), 1).astype(f32)
+
+    def picked(r, weights):
+        here = slice(r * BLOCK, (r + 1) * BLOCK)
+        picks = (neurons == chosen[:, here].T[:, 0:1]).astype(f32).astype(bf16)
+        return jnp.dot(picks, weights[...], preferred_element_type=f32)
+
+    for r in range(slots // BLOCK):
+        hot_in[:, r * BLOCK : (r + 1) * BLOCK] = picked(r, win).T.astype(bf16)
     load_out.wait()
-
-    @pl.loop(0, slots // BLOCK)
-    def _(r):
-        here = pl.ds(pl.multiple_of(r * BLOCK, BLOCK), BLOCK)
-        chosen = (
-            lax.broadcasted_iota(jnp.int32, (BLOCK, hidden), 1) == col_ref[here, :]
-        ).astype(f32).astype(bf16)
-        hot_out_ref[here, :] = jnp.dot(chosen, wout[...], preferred_element_type=f32).astype(bf16)
+    for r in range(slots // BLOCK):
+        hot_out_ref[r * BLOCK : (r + 1) * BLOCK, :] = picked(r, wout).astype(bf16)
 
     for lv in range(1, up):
 
@@ -204,8 +200,9 @@
             arrive(o, None)
     row = lax.broadcasted_iota(jnp.int32, (rows, rows), 0)
     col = lax.broadcasted_iota(jnp.int32, (rows, rows), 1)
+    mine = jnp.broadcast_to(doc_ref[...].astype(f32), (128, rows)).T[:, 0:1]
     for o in range(window + 1):
-        seen = qdoc_ref[...] == docs[o, 0:1, :]
+        seen = mine == docs[o].astype(f32)
         if o == 0:
             seen = seen & (row >= col)
         bias[o] = jnp.where(seen, 0.0, masked_score)
@@ -237,6 +234,13 @@
                 accum = term if accum is None else accum + term
             attended[:, here] = (accum[:, :HEAD_DIM] / accum[:, HEAD_DIM:]).astype(bf16)
 
+    shared = []
+    for d in range(1, ny):
+        shared.append(remote(
+            hot_in, all_ref.at[:, pl.ds(d * slots, slots)], w_s.at[d - 1], w_r.at[d - 1],
+            (z * ny + (y + ny - d) % ny, me),
+        ))
+
     @pl.loop(0, count + 1)
     def _(i):
         @pl.when(i < count)
@@ -244,18 +248,15 @@
             arrive(up * ny, i)
             spread(up, i, start)
 
+        @pl.when(i == count - 1)
+        def _():
+            for copy in shared:
+                copy.start()
+
         @pl.when(i > 0)
         def _():
             attend(i - 1)
 
-    shared = []
-    for d in range(1, ny):
-        copy = remote(
-            hot_in, all_ref.at[:, pl.ds(d * slots, slots)], w_s.at[d - 1], w_r.at[d - 1],
-            (z * ny + (y + ny - d) % ny, me),
-        )
-        copy.start()
-        shared.append(copy)
     own = pltpu.make_async_copy(hot_in, all_ref.at[:, pl.ds(0, slots)], own_sem)
     own.start()
     load_proj.wait()
@@ -356,7 +357,7 @@
     own.wait()
 
 
-def front(queries, keys, values, doc_ids, resid, gain, chosen, w_in, w_out, out_proj, ny, collective_id):
+def front(queries, keys, values, doc_ids, resid, gain, index, live, w_in, w_out, out_proj, ny, collective_id):
     rows, width = queries.shape
     n = lax.axis_size("seq")
     nmp = lax.axis_size("mp")
@@ -367,7 +368,7 @@
     heads = width // HEAD_DIM
     per = 2 if heads % 2 == 0 else 1
     pieces = 1 + 2 * (heads // per)
-    slots = chosen.shape[0]
+    slots = index.shape[1]
     parts = 2
     band = rows // parts
     dma = pltpu.SemaphoreType.DMA
@@ -375,7 +376,6 @@
     anywhere = pl.BlockSpec(memory_space=pl.ANY)
     f32 = jnp.float32
     bf16 = jnp.bfloat16
-    doc_row = jnp.broadcast_to(doc_ids[None, :], (8, rows))
     return pl.pallas_call(
         functools.partial(front_kernel, nz, ny, nmp, up, window, per, HEAD_DIM ** (-0.5)),
         out_shape=[
@@ -384,17 +384,17 @@
             jax.ShapeDtypeStruct((width, ny * slots), bf16),
             jax.ShapeDtypeStruct((slots, width), bf16),
         ],
-        in_specs=[vmem] * 9 + [anywhere] * 3,
+        in_specs=[vmem] * 7 + [pl.BlockSpec(memory_space=pltpu.SMEM)] + [anywhere] * 3,
         out_specs=[vmem, vmem, anywhere, vmem],
         scratch_shapes=[
             VMEM((window, rows, width), bf16),
             VMEM((window, rows, width), bf16),
-            VMEM((window + 1, 8, rows), jnp.int32),
+            VMEM((window + 1, 1, rows), jnp.int32),
             VMEM((window + 1, rows, rows), f32),
             VMEM((per, window + 1, rows, rows), f32),
             VMEM((rows, width), bf16),
             VMEM(out_proj.shape, bf16),
-            VMEM(w_in.shape, bf16),
+            VMEM(w_in.shape[::-1], bf16),
             VMEM(w_out.shape, bf16),
             VMEM((width, slots), bf16),
             VMEM((chips - 1, parts, band, width), bf16),
@@ -425,8 +425,7 @@
             collective_id=collective_id, has_side_effects=True, vmem_limit_bytes=63 * 1024 * 1024
         ),
     )(
-        queries, keys, values, doc_row, doc_ids[:, None], resid, gain[None, :],
-        chosen[None, :], chosen[:, None], w_in, w_out, out_proj,
+        queries, keys, values, doc_ids[None, :], resid, gain[None, :], index, live, w_in.T, w_out, out_proj,
     )
 
 
@@ -797,11 +796,8 @@
 ):
     rows = resid.shape[0]
     total_tokens = rows * lax.axis_size("seq")
-    slots = hot_index.shape[1]
-    live = jnp.arange(slots, dtype=jnp.int32) < BLOCK * hot_blocks[0]
-    chosen = jnp.where(live, hot_index[0], -1)
     state, normed, win, hot_out = front(
-        queries, keys, values, doc_ids, resid, ffn_gain, chosen, w_in, w_out, out_proj, ny, 0
+        queries, keys, values, doc_ids, resid, ffn_gain, hot_index, hot_blocks, w_in, w_out, out_proj, ny, 0
     )
     return ffn(normed, state, win, hot_out, ny, 4, total_tokens, 1)
 

time: 210 us -> 194 us (0.924)
  local copies, waits for them, and re-layouts: 15.2 us -> 4.45 us
  Pallas kernels: 191 us -> 188 us
    unnamed x3 -> x2, local copies, waits for them, and re-layouts: 10.3 us -> 3.17 us
    pallas_call x1, Pallas kernels: 61.5 us -> 56.9 us  [front(): pl.pallas_call(functools.partial(front_kernel, nz, ny, nmp, up, window, p...]
    broadcast_in_dim x2 -> x0, local copies, waits for them, and re-layouts: 2.75 us -> none  [the longest x1 1.47 us: front(): doc_ids[:, None]]
where the time goes in v3:
time: 194 us
  Pallas kernels  188 us (97%)
  local copies, waits for them, and re-layouts  4.45 us (2%)
    pallas_call x1, Pallas kernels, ffn(): pl.pallas_call(functools.partial(ffn_kernel, nz, ny, nmp, count, total_to...  131 us
    pallas_call x1, Pallas kernels, front(): pl.pallas_call(functools.partial(front_kernel, nz, ny, nmp, up, window, p...  56.9 us

profile of v3, /device:TPU:0, one launch (start us, length us, event | category | flops | bytes accessed | tf_op | source)
XLA Modules:
  0.0 194.1 jit_solution(7959667453283263851)
XLA Ops:
  1.3 1.3 broadcast_in_dim.7.gain_ref
  2.6 56.9 %shard_map.122 = (bf16[256,1280]{1,0:T(8,128)(2,1)}, bf16[256,1280]{1,0:T(8,128)(2,1)}, bf16[1280,768]{1,0:T(8,128)(2,1)}, bf16[384,1280]{1,0:T(8,128)(2,1)}) custom-call(bf16[256,1280]{1,0:T(8,128)(2,1)} %q_ref.1, bf16[256,1280]{1,0:T(8,128)(2,1)} %k_ref.1, bf16[256,1280]{1,0:T(8,128)(2,1)} %v_ref.1, s32[1,256]{1,0:T(1,128)} %bitcast.3, ...), custom_call_target="tpu_custom_call" | custom-call | tf_op jit(solution)/shard_map/pallas_call | solution.py:379
  59.5 131.4 %shard_map.123 = (bf16[256,1280]{1,0:T(8,128)(2,1)}, f32[1,384]{1,0:T(1,128)}) custom-call(bf16[256,1280]{1,0:T(8,128)(2,1)} %get-tuple-element.6.x_ref, bf16[256,1280]{1,0:T(8,128)(2,1)} %get-tuple-element.7.state_ref, bf16[1280,768]{1,0:T(8,128)(2,1)} %get-tuple-element.8.win_ref, bf16[384,1280]{1,0:T(8,128)(2,1)} %get-tuple-element.9.wout_ref), custom_call_target="tpu_custom_call" | custom-call | tf_op jit(solution)/shard_map/pallas_call | solution.py:732
  190.9 2.0 %copy.16 = bf16[256,1280]{1,0:T(8,128)(2,1)} copy(bf16[256,1280]{1,0:T(8,128)(2,1)} %get-tuple-element.12) | data formatting | bytes 1310720
  192.9 1.2 copy.17

commit v4 on v3

v4 whole, which is shorter than its diff:
```python
import functools

import jax
import jax.numpy as jnp
from jax import lax
from jax.experimental import pallas as pl
from jax.experimental.pallas import tpu as pltpu
from jax.sharding import PartitionSpec as P

HEAD_DIM = 128
BLOCK = 128
MESH = pl.DeviceIdType.MESH
VMEM = pltpu.VMEM

epsilon = 1e-05
masked_score = -1e30


def row_length(mesh):
    seq = mesh.shape["seq"]
    try:
        first = [mesh.devices[i, 0].coords for i in range(seq)]
        size = len({c[1] for c in first})
        if seq % size == 0:
            return size
    except (AttributeError, IndexError, TypeError):
        pass
    return 2


def ffn_order(nz, count):
    period = 42.0 / count
    timed = []

    def put(at, stage, distance=0):
        for c in range(count):
            timed.append((at + period * c, len(timed), stage, distance, c))

    put(-16.3, "own")
    for k in range(1, nz):
        put(-5.0 + 4.5 * k, "collect", k)
    arrived = -5.0 + 4.5 * (nz - 1)
    put(arrived, "multiply_in")
    put(11.7, "exchange")
    put(18.4, "activate")
    put(22.1, "multiply_out")
    for k in range(nz - 1, 0, -1):
        put(max(38.5 - 4.5 * k, 22.1) if k < nz - 1 else 22.1, "middle", k)
    put(1000.0, "finish")
    return [entry[2:] for entry in sorted(timed)]


def layer_kernel(
    nz, ny, nmp, up, window, per, count, scale, total_tokens,
    q_ref, k_ref, v_ref, doc_ref, resid_ref, gain_ref, index_ref, live_ref, win_hbm, wout_hbm, proj_hbm,
    out_ref, mean_ref,
    kbuf, vbuf, docs, bias, scores, attended, proj, weights, win, wout,
    far_part, far_near, sums, far, near_part, near_near, total, squares, state, normed,
    gathered, part, own_part, near, pair, active, contrib, from_below, from_above,
    hot, hot_near, hot_send, hot_other,
    load_sem, z_s, y_s, recv, f_s, f_r, near_s, near_r, x_s, x_r, q_s, q_r, wi_s, wi_r, wo_s, wo_r,
    ag_s, ag_r, pd_s, pd_r, px_s, px_r, ad_s, ad_r, up_s, up_r, dn_s, dn_r, hp_s, hp_r, hy_s, hy_r,
):
    f32 = jnp.float32
    bf16 = jnp.bfloat16
    seq = lax.axis_index("seq")
    me = lax.axis_index("mp")
    z = seq // ny
    y = seq % ny
    chips = nmp // 2
    chip = me // 2
    core = me % 2
    rows, width = q_ref.shape
    wide = per * HEAD_DIM
    groups = width // wide
    slots = index_ref.shape[1]
    last = nz - 1
    partner = (seq, chip * 2 + 1 - core)

    barrier = pltpu.get_barrier_semaphore()

    def greet(where):
        pl.semaphore_signal(barrier, inc=1, device_id=where, device_id_type=MESH)

    above = ((z + 1) * ny + y, me)

    @pl.when(z > 0)
    def _():
        greet(((z - 1) * ny + y, me))

    @pl.when(z < last)
    def _():
        greet(above)

    for d in range(1, nmp):
        greet((seq, (me + d) % nmp))
    for d in range(1, ny):
        greet((z * ny + (y + d) % ny, me))
    has_below = jnp.where(z > 0, 1, 0)
    has_above = jnp.where(z < last, 1, 0)
    pl.semaphore_wait(barrier, has_below + has_above + nmp + ny - 2)

    def remote(src, dst, send, got, where):
        return pltpu.make_async_remote_copy(
            src_ref=src, dst_ref=dst, send_sem=send, recv_sem=got,
            device_id=where, device_id_type=MESH,
        )

    def cols(c):
        return pl.ds(pl.multiple_of(c * wide, 128), wide)

    def pieces(lv, c):
        slot = lv * ny - 1
        if lv == 0:
            return k_ref.at[:, cols(c)], v_ref.at[:, cols(c)]
        return kbuf.at[slot, :, cols(c)], vbuf.at[slot, :, cols(c)]

    def landing(o, c):
        return kbuf.at[o - 1, :, cols(c)], vbuf.at[o - 1, :, cols(c)]

    def copies(lv, o, c, send, where):
        if c is None:
            src = doc_ref if lv == 0 else docs.at[lv * ny]
            return [remote(src, docs.at[o], send.at[0], recv.at[o, 0], where)]
        out = []
        for j, (src, dst) in enumerate(zip(pieces(lv, c), landing(o, c))):
            p = 1 + 2 * c + j
            out.append(remote(src, dst, send.at[p], recv.at[o, p], where))
        return out

    def z_copies(lv, c):
        return copies(lv, (lv + 1) * ny, c, z_s.at[lv], above)

    def y_copies(lv, d, c):
        other = (y + d) % ny
        return copies(lv, lv * ny + other - y, c, y_s.at[lv, d - 1], (z * ny + other, me))

    def holds(lv):
        return z >= lv

    def y_wanted(lv, d):
        o = lv * ny + (y + d) % ny - y
        return holds(lv) & (o >= 0) & (o <= window)

    def spread(lv, c, act):
        if lv < up:

            @pl.when(holds(lv) & (z < last))
            def _():
                for copy in z_copies(lv, c):
                    act(copy)

        for d in range(1, ny):

            @pl.when(y_wanted(lv, d))
            def _(d=d):
                for copy in y_copies(lv, d, c):
                    act(copy)

    def start(copy):
        copy.start()

    def arrive(o, c):
        @pl.when(seq >= o)
        def _():
            if c is None:
                remote(docs.at[o], docs.at[o], z_s.at[0, 0], recv.at[o, 0], partner).wait_recv()
                return
            for j, dst in enumerate(landing(o, c)):
                p = 1 + 2 * c + j
                remote(dst, dst, z_s.at[0, p], recv.at[o, p], partner).wait_recv()

    spread(0, None, start)
    spread(0, 0, start)
    load_in = pltpu.make_async_copy(win_hbm, weights, load_sem.at[0])
    load_in.start()
    load_proj = pltpu.make_async_copy(proj_hbm, proj, load_sem.at[2])
    load_proj.start()
    for o in range(1, window + 1):

        @pl.when(seq < o)
        def _(o=o):
            kbuf[o - 1] = jnp.zeros((rows, width), bf16)
            vbuf[o - 1] = jnp.zeros((rows, width), bf16)
            docs[o] = jnp.full(docs.shape[1:], -1, jnp.int32)

    docs[0] = doc_ref[...]
    arrive(ny, None)
    spread(1, None, start)
    for c in range(1, groups):
        spread(0, c, start)

    load_in.wait()
    hidden = weights.shape[0]
    order = lax.broadcasted_iota(jnp.int32, (1, slots), 1)
    chosen = jnp.where(order < BLOCK * live_ref[0], index_ref[...], -1).astype(f32)
    chosen = jnp.broadcast_to(chosen, (BLOCK, slots))
    neurons = lax.broadcasted_iota(jnp.int32, (BLOCK, hidden), 1).astype(f32)

    def picked(r):
        here = slice(r * BLOCK, (r + 1) * BLOCK)
        picks = (neurons == chosen[:, here].T[:, 0:1]).astype(f32).astype(bf16)
        return jnp.dot(picks, weights[...], preferred_element_type=f32)

    for r in range(slots // BLOCK):
        win[:, r * BLOCK : (r + 1) * BLOCK] = picked(r).T.astype(bf16)
    load_out = pltpu.make_async_copy(wout_hbm, weights, load_sem.at[1])
    load_out.start()
    load_out.wait()
    for r in range(slots // BLOCK):
        wout[r * BLOCK : (r + 1) * BLOCK, :] = picked(r).astype(bf16)

    for lv in range(1, up):

        @pl.loop(0, groups)
        def _(c, lv=lv):
            arrive(lv * ny, c)
            spread(lv, c, start)

    for lv in range(2, up + 1):
        arrive(lv * ny, None)
        spread(lv, None, start)
    for o in range(1, window + 1):
        if o % ny:
            arrive(o, None)
    row = lax.broadcasted_iota(jnp.int32, (rows, rows), 0)
    col = lax.broadcasted_iota(jnp.int32, (rows, rows), 1)
    mine = jnp.broadcast_to(doc_ref[...].astype(f32), (128, rows)).T[:, 0:1]
    for o in range(window + 1):
        seen = mine == docs[o].astype(f32)
        if o == 0:
            seen = seen & (row >= col)
        bias[o] = jnp.where(seen, 0.0, masked_score)

    factor = scale * 1.4426950408889634

    def attend(c):
        for o in range(1, window + 1):
            if o % ny:
                arrive(o, c)
        for h in range(per):
            here = pl.ds(pl.multiple_of(c * wide + h * HEAD_DIM, HEAD_DIM), HEAD_DIM)
            query = q_ref[:, here]
            top = None
            for o in range(window + 1):
                key = k_ref[:, here] if o == 0 else kbuf[o - 1, :, here]
                score = lax.dot_general(
                    query, key, (((1,), (1,)), ((), ())), preferred_element_type=f32
                ) + bias[o]
                scores[h, o] = score
                top = score if top is None else jnp.maximum(top, score)
            peak = jnp.max(top, axis=1, keepdims=True)
            accum = None
            for o in range(window + 1):
                value = v_ref[:, here] if o == 0 else vbuf[o - 1, :, here]
                both = jnp.concatenate([value, jnp.ones((rows, HEAD_DIM), bf16)], axis=1)
                weight = jnp.exp2((scores[h, o] - peak) * factor).astype(bf16)
                term = jnp.dot(weight, both, preferred_element_type=f32)
                accum = term if accum is None else accum + term
            attended[:, here] = (accum[:, :HEAD_DIM] / accum[:, HEAD_DIM:]).astype(bf16)

    def win_copy(d):
        return remote(
            win.at[:, pl.ds(0, slots)], win.at[:, pl.ds(d * slots, slots)],
            wi_s.at[d - 1], wi_r.at[d - 1], (z * ny + (y + ny - d) % ny, me),
        )

    def wout_copy(d):
        return remote(
            wout.at[pl.ds(0, slots)], wout.at[pl.ds(d * slots, slots)],
            wo_s.at[d - 1], wo_r.at[d - 1], (z * ny + (y + ny - d) % ny, me),
        )

    @pl.loop(0, groups + 1)
    def _(i):
        @pl.when(i < groups)
        def _():
            arrive(up * ny, i)
            spread(up, i, start)

        @pl.when(i == groups - 1)
        def _():
            for d in range(1, ny):
                win_copy(d).start()
            for d in range(1, ny):
                wout_copy(d).start()

        @pl.when(i > 0)
        def _():
            attend(i - 1)

    def at_z(step):
        return ((z + step) * ny + y, me)

    def at_y(d):
        return (z * ny + (y + d) % ny, me)

    def at_x(d):
        return (seq, ((chip + d) % chips) * 2 + core)

    load_proj.wait()

    size = rows // count
    half = nz // 2
    span = half * size
    parts = near_s.shape[0]
    band = rows // parts

    def block(r, target, side):
        where = pl.ds(pl.multiple_of((target * 2 + side) * width, 128), width)
        return jnp.dot(
            attended[r * band : (r + 1) * band, :], proj[:, where], preferred_element_type=f32
        )

    def far_copy(d, r):
        here = pl.ds(r * band, band)
        return remote(
            far_part.at[d - 1, here], far_near.at[d - 1, here], f_s.at[d - 1, r], f_r.at[d - 1, r],
            partner,
        )

    def cross_copy(d, c):
        here = pl.ds(c * size, size)
        return remote(
            sums.at[d - 1, here], far.at[d - 1, here], x_s.at[d - 1, c], x_r.at[d - 1, c],
            (seq, ((chip + d) % chips) * 2 + core),
        )

    def near_copy(r):
        here = pl.ds(r * band, band)
        return remote(near_part.at[here], near_near.at[here], near_s.at[r], near_r.at[r], partner)

    def square_copy(d, c):
        return remote(
            squares.at[c, me], squares.at[c, me], q_s.at[d - 1, c], q_r.at[me, c],
            (seq, (me + d) % nmp),
        )

    for r in range(parts):
        here = slice(r * band, (r + 1) * band)
        for d in range(1, chips):
            far_part[d - 1, here] = block(r, (chip + d) % chips, 1 - core).astype(bf16)
            far_copy(d, r).start()
        for d in range(1, chips):
            mine = block(r, (chip + d) % chips, core)
            far_copy(d, r).wait_recv()
            sums[d - 1, here] = (mine + far_near[d - 1, here].astype(f32)).astype(bf16)
            for c in range(r * band // size, (r + 1) * band // size):
                cross_copy(d, c).start()
    for r in range(parts):
        here = slice(r * band, (r + 1) * band)
        near_part[here, :] = block(r, chip, 1 - core).astype(bf16)
        near_copy(r).start()
        mine = block(r, chip, core)
        near_copy(r).wait_recv()
        total[here, :] = resid_ref[here, :].astype(f32) + (mine + near_near[here, :].astype(f32))

    def settle(c):
        here = slice(c * size, (c + 1) * size)
        value = total[here, :]
        for d in range(1, chips):
            cross_copy(d, c).wait_recv()
            value = value + far[d - 1, here].astype(f32)
        value = value.astype(bf16)
        state[here, :] = value
        widened = value.astype(f32)
        length = jnp.sum(widened * widened, axis=1, keepdims=True)
        flat = jnp.broadcast_to(length, (size, 128)).T[0:8, :]
        squares[c, me] = jnp.concatenate([flat] * (128 // size), axis=1)
        for d in range(1, nmp):
            square_copy(d, c).start()

    def normalize(c):
        here = slice(c * size, (c + 1) * size)
        for d in range(1, nmp):
            other = (me + d) % nmp
            remote(
                squares.at[c, other], squares.at[c, other], q_s.at[d - 1, c], q_r.at[other, c],
                partner,
            ).wait_recv()
        square = squares[c, 0]
        for k in range(1, nmp):
            square = square + squares[c, k]
        inverse = lax.rsqrt(square / (width * nmp) + epsilon)
        column = jnp.broadcast_to(inverse[0:1, 0:size], (128, size)).T[:, 0:1]
        normed[here, :] = (
            state[here, :].astype(f32) * column * gain_ref[...].astype(f32)
        ).astype(bf16)

    def own_rows(c):
        return normed.at[pl.ds(c * size, size)]

    def gather_copy(step, k, c):
        block = z - step * k
        src = own_rows(c) if k == 0 else gathered.at[c, block]
        way = 0 if step > 0 else 1
        return remote(src, gathered.at[c, block], ag_s.at[way, k, c], ag_r.at[block, c], at_z(step))

    def can_pass(step, k):
        block = z - step * k
        there = z + step
        return (block >= 0) & (block < nz) & (there >= 0) & (there < nz)

    def pass_on(k, c, steps=(1, -1)):
        for step in steps:

            @pl.when(can_pass(step, k))
            def _(step=step):
                gather_copy(step, k, c).start()

    def own_send(c):
        normalize(c)
        pass_on(0, c)

    def collect(k, c):
        if k == 1:
            gathered[c, z] = normed[pl.ds(c * size, size), :]
        for step in (1, -1):
            block = z - step * k

            @pl.when((block >= 0) & (block < nz))
            def _(step=step, block=block):
                remote(
                    gathered.at[c, block], gathered.at[c, block],
                    ag_s.at[0, 0, c], ag_r.at[block, c], partner,
                ).wait_recv()
                if k < nz - 1:
                    pass_on(k, c, (step,))

    def half_rows(side):
        return pl.ds(side * half, half)

    def pre_copy(c):
        return remote(part.at[c], near.at[c], pd_s.at[c], pd_r.at[c], partner)

    def multiply_in(c):
        other = gathered[c, half_rows(1 - core)].reshape(span, width)
        part[c] = jnp.dot(other, win[...], preferred_element_type=f32).astype(bf16)
        pre_copy(c).start()
        mine = gathered[c, half_rows(core)].reshape(span, width)
        own_part[c] = jnp.dot(mine, win[...], preferred_element_type=f32)

    def across_copy(d, c):
        return remote(
            pair.at[c, chip], pair.at[c, chip], px_s.at[d - 1, c], px_r.at[chip, c], at_x(d)
        )

    def exchange(c):
        pre_copy(c).wait_recv()
        pair[c, chip] = (own_part[c] + near[c].astype(f32)).astype(bf16)
        for d in range(1, chips):
            across_copy(d, c).start()

    def active_copy(c):
        return remote(
            active.at[c, half_rows(core)], active.at[c, half_rows(core)],
            ad_s.at[c], ad_r.at[c], partner,
        )

    def activate(c):
        for d in range(1, chips):
            other = (chip + d) % chips
            remote(
                pair.at[c, other], pair.at[c, other], px_s.at[d - 1, c], px_r.at[other, c], at_x(d)
            ).wait_recv()
        pre = pair[c, 0].astype(f32)
        for k in range(1, chips):
            pre = pre + pair[c, k].astype(f32)
        value = jnp.maximum(pre, 0.0)
        active[c, half_rows(core)] = value.astype(bf16).reshape(half, size, value.shape[1])
        active_copy(c).start()
        hot[...] += jnp.sum(value.reshape(span // 8, 8, value.shape[1]), axis=0)

    def up_copy(t, c):
        return remote(from_below.at[c, t], from_below.at[c, t], up_s.at[t, c], up_r.at[t, c], at_z(1))

    def down_copy(t, c):
        return remote(from_above.at[c, t], from_above.at[c, t], dn_s.at[t, c], dn_r.at[t, c], at_z(-1))

    def multiply_out(c):
        other = half_rows(1 - core)
        remote(active.at[c, other], active.at[c, other], ad_s.at[c], ad_r.at[c], partner).wait_recv()
        lhs = active[c].reshape(nz * size, active.shape[3])
        contrib[c] = jnp.dot(lhs, wout[...], preferred_element_type=f32).reshape(nz, size, width)

        @pl.when(z == 0)
        def _():
            for t in range(last, 0, -1):
                from_below[c, t] = contrib[c, t].astype(bf16)
                up_copy(t, c).start()

        @pl.when(z == last)
        def _():
            for t in range(last):
                from_above[c, t] = contrib[c, t].astype(bf16)
                down_copy(t, c).start()

    def middle(k, c):
        up = z + k

        @pl.when((z > 0) & (up < nz))
        def _():
            up_copy(up, c).wait_recv()
            from_below[c, up] = (contrib[c, up] + from_below[c, up].astype(f32)).astype(bf16)
            up_copy(up, c).start()

        down = z - k

        @pl.when((z < last) & (down >= 0))
        def _():
            down_copy(down, c).wait_recv()
            from_above[c, down] = (contrib[c, down] + from_above[c, down].astype(f32)).astype(bf16)
            down_copy(down, c).start()

    def finish(c):
        @pl.when(z > 0)
        def _():
            up_copy(z, c).wait_recv()
            contrib[c, z] += from_below[c, z].astype(f32)

        @pl.when(z < last)
        def _():
            down_copy(z, c).wait_recv()
            contrib[c, z] += from_above[c, z].astype(f32)

        here = pl.ds(c * size, size)
        out_ref[here, :] = (state[here, :].astype(f32) + contrib[c, z]).astype(bf16)

    hot[...] = jnp.zeros_like(hot)
    eager = min(2, count)
    for c in range(eager):
        settle(c)
        own_send(c)
    for c in range(eager, count):
        settle(c)
    for stage, k, c in ffn_order(nz, count):
        if stage == "own":
            if c >= eager:
                own_send(c)
        elif stage == "collect":
            collect(k, c)
        elif stage == "multiply_in":
            if c == 0:
                for d in range(1, ny):
                    win_copy(d).wait_recv()
            multiply_in(c)
        elif stage == "exchange":
            exchange(c)
        elif stage == "activate":
            activate(c)
        elif stage == "multiply_out":
            if c == 0:
                for d in range(1, ny):
                    wout_copy(d).wait_recv()
            multiply_out(c)
        elif stage == "middle":
            middle(k, c)

    hot_pair = remote(hot, hot_near, hp_s, hp_r, partner)
    hot_pair.start()
    hot_pair.wait_recv()
    both = jnp.sum(hot[...] + hot_near[...], axis=0, keepdims=True)
    hot_send[...] = jnp.broadcast_to(both, hot_send.shape)

    def mean_copy(d):
        return remote(
            hot_send.at[:, pl.ds(d * slots, slots)], hot_other.at[d - 1],
            hy_s.at[d - 1], hy_r.at[d - 1], at_y(d),
        )

    for d in range(1, ny):
        mean_copy(d).start()
    for c in range(count):
        finish(c)
    total = hot_send[0:1, 0:slots]
    for d in range(1, ny):
        mean_copy(d).wait_recv()
        total = total + hot_other[d - 1, 0:1, :]
    mean_ref[...] = total / total_tokens

    for c in range(count):
        for k in range(nz - 1):
            for step in (1, -1):

                @pl.when(can_pass(step, k))
                def _(step=step, k=k, c=c):
                    gather_copy(step, k, c).wait_send()

        pre_copy(c).wait_send()
        for d in range(1, chips):
            across_copy(d, c).wait_send()
        active_copy(c).wait_send()
        for t in range(nz):

            @pl.when((t > z) & (z < last))
            def _(t=t, c=c):
                up_copy(t, c).wait_send()

            @pl.when((t < z) & (z > 0))
            def _(t=t, c=c):
                down_copy(t, c).wait_send()

    for d in range(1, ny):
        win_copy(d).wait_send()
        wout_copy(d).wait_send()
        mean_copy(d).wait_send()
    hot_pair.wait_send()
    for lv in range(up + 1):
        spread(lv, None, lambda copy: copy.wait_send())

        @pl.loop(0, groups)
        def _(c, lv=lv):
            spread(lv, c, lambda copy: copy.wait_send())

    for d in range(1, chips):
        for r in range(parts):
            far_copy(d, r).wait_send()
        for c in range(count):
            cross_copy(d, c).wait_send()
    for r in range(parts):
        near_copy(r).wait_send()
    for d in range(1, nmp):
        for c in range(count):
            square_copy(d, c).wait_send()


def layer(queries, keys, values, doc_ids, resid, gain, index, live, w_in, w_out, out_proj, ny, count, collective_id):
    rows, width = queries.shape
    n = lax.axis_size("seq")
    nmp = lax.axis_size("mp")
    nz = n // ny
    chips = nmp // 2
    window = n // 2
    up = min(nz - 1, -(-window // ny))
    heads = width // HEAD_DIM
    per = 2 if heads % 2 == 0 else 1
    pieces = 1 + 2 * (heads // per)
    slots = index.shape[1]
    parts = 2
    size = rows // count
    span = (nz // 2) * size
    wide = ny * slots
    dma = pltpu.SemaphoreType.DMA
    vmem = pl.BlockSpec(memory_space=VMEM)
    anywhere = pl.BlockSpec(memory_space=pl.ANY)
    f32 = jnp.float32
    bf16 = jnp.bfloat16
    return pl.pallas_call(
        functools.partial(
            layer_kernel, nz, ny, nmp, up, window, per, count, HEAD_DIM ** (-0.5), n * rows
        ),
        out_shape=[
            jax.ShapeDtypeStruct((rows, width), bf16),
            jax.ShapeDtypeStruct((1, slots), f32),
        ],
        in_specs=[vmem] * 7 + [pl.BlockSpec(memory_space=pltpu.SMEM)] + [anywhere] * 3,
        out_specs=[vmem, vmem],
        scratch_shapes=[
            VMEM((window, rows, width), bf16),
            VMEM((window, rows, width), bf16),
            VMEM((window + 1, 1, rows), jnp.int32),
            VMEM((window + 1, rows, rows), f32),
            VMEM((per, window + 1, rows, rows), f32),
            VMEM((rows, width), bf16),
            VMEM(out_proj.shape, bf16),
            VMEM(w_out.shape, bf16),
            VMEM((width, wide), bf16),
            VMEM((wide, width), bf16),
            VMEM((chips - 1, rows, width), bf16),
            VMEM((chips - 1, rows, width), bf16),
            VMEM((chips - 1, rows, width), bf16),
            VMEM((chips - 1, rows, width), bf16),
            VMEM((rows, width), bf16),
            VMEM((rows, width), bf16),
            VMEM((rows, width), f32),
            VMEM((count, nmp, 8, 128), f32),
            VMEM((rows, width), bf16),
            VMEM((rows, width), bf16),
            VMEM((count, nz, size, width), bf16),
            VMEM((count, span, wide), bf16),
            VMEM((count, span, wide), f32),
            VMEM((count, span, wide), bf16),
            VMEM((count, chips, span, wide), bf16),
            VMEM((count, nz, size, wide), bf16),
            VMEM((count, nz, size, width), f32),
            VMEM((count, nz, size, width), bf16),
            VMEM((count, nz, size, width), bf16),
            VMEM((8, wide), f32),
            VMEM((8, wide), f32),
            VMEM((8, wide), f32),
            VMEM((ny - 1, 8, slots), f32),
            dma((3,)),
            dma((up, pieces)),
            dma((up + 1, ny - 1, pieces)),
            dma((window + 1, pieces)),
            dma((chips - 1, parts)),
            dma((chips - 1, parts)),
            dma((parts,)),
            dma((parts,)),
            dma((chips - 1, count)),
            dma((chips - 1, count)),
            dma((nmp - 1, count)),
            dma((nmp, count)),
            dma((ny - 1,)),
            dma((ny - 1,)),
            dma((ny - 1,)),
            dma((ny - 1,)),
            dma((2, nz, count)),
            dma((nz, count)),
            dma((count,)),
            dma((count,)),
            dma((chips - 1, count)),
            dma((chips, count)),
            dma((count,)),
            dma((count,)),
            dma((nz, count)),
            dma((nz, count)),
            dma((nz, count)),
            dma((nz, count)),
            dma,
            dma,
            dma((ny - 1,)),
            dma((ny - 1,)),
        ],
        compiler_params=pltpu.CompilerParams(
            collective_id=collective_id, has_side_effects=True, vmem_limit_bytes=67043328
        ),
    )(
        queries, keys, values, doc_ids[None, :], resid, gain[None, :], index, live, w_in.T, w_out, out_proj,
    )


def local(
    ny,
    resid,
    queries,
    keys,
    values,
    doc_ids,
    out_proj,
    ffn_gain,
    w_in,
    w_out,
    hot_index,
    hot_blocks,
):
    return layer(
        queries, keys, values, doc_ids, resid, ffn_gain, hot_index, hot_blocks, w_in, w_out, out_proj, ny, 4, 0
    )


def solution(mesh):
    return jax.shard_map(
        functools.partial(local, row_length(mesh)),
        mesh=mesh,
        in_specs=(
            P("seq", "mp"),
            P("seq", "mp"),
            P("seq", "mp"),
            P("seq", "mp"),
            P("seq"),
            P("mp", None),
            P("mp"),
            P("mp", "seq"),
            P("seq", "mp"),
            P("seq", None),
            P("seq"),
        ),
        out_specs=(P("seq", "mp"), P("seq", None)),
        check_vma=False,
    )
```

time: 194 us -> 181 us (0.933)
  Pallas kernels: 188 us -> 175 us
    pallas_call x2 -> x1, Pallas kernels: 188 us -> 175 us  [layer(): pl.pallas_call(functools.partial(layer_kernel, nz, ny, nmp, up, window, p...]
where the time goes in v4:
time: 181 us
  Pallas kernels  175 us (97%)
  local copies, waits for them, and re-layouts  4.47 us (2%)
    pallas_call x1, Pallas kernels, layer(): pl.pallas_call(functools.partial(layer_kernel, nz, ny, nmp, up, window, p...  175 us

profile of v4, /device:TPU:0, one launch (start us, length us, event | category | flops | bytes accessed | tf_op | source)
XLA Modules:
  0.0 180.9 jit_solution(1669671204062590420)
XLA Ops:
  1.3 1.3 broadcast_in_dim.7.gain_ref
  2.6 175.1 %shard_map.122 = (bf16[256,1280]{1,0:T(8,128)(2,1)}, f32[1,384]{1,0:T(1,128)}) custom-call(bf16[256,1280]{1,0:T(8,128)(2,1)} %q_ref.1, bf16[256,1280]{1,0:T(8,128)(2,1)} %k_ref.1, bf16[256,1280]{1,0:T(8,128)(2,1)} %v_ref.1, s32[1,256]{1,0:T(1,128)} %bitcast.3, bf16[256,1280]{1,0:T(8,128)(2,1)} %resid_ref.1, bf16[1,1280]{1,0:T(2,128)(2,1)} %broadcast_in_dim.7.gain_ref, ...), custom_call_target="tpu_custom_call" | custom-call | tf_op jit(solution)/shard_map/pallas_call | solution.py:648
  177.7 2.0 %copy.16 = bf16[256,1280]{1,0:T(8,128)(2,1)} copy(bf16[256,1280]{1,0:T(8,128)(2,1)} %get-tuple-element.4) | data formatting | bytes 1310720
  179.7 1.2 copy.17

commit v5 on v4

--- a/solution.py
+++ b/solution.py
@@ -51,11 +51,11 @@
 
 
 def layer_kernel(
-    nz, ny, nmp, up, window, per, count, scale, total_tokens,
+    nz, ny, nmp, up, window, per, count, scale,
     q_ref, k_ref, v_ref, doc_ref, resid_ref, gain_ref, index_ref, live_ref, win_hbm, wout_hbm, proj_hbm,
-    out_ref, mean_ref,
+    state, delta_ref, mean_ref,
     kbuf, vbuf, docs, bias, scores, attended, proj, weights, win, wout,
-    far_part, far_near, sums, far, near_part, near_near, total, squares, state, normed,
+    far_part, far_near, sums, far, near_part, near_near, total, squares, normed,
     gathered, part, own_part, near, pair, active, contrib, from_below, from_above,
     hot, hot_near, hot_send, hot_other,
     load_sem, z_s, y_s, recv, f_s, f_r, near_s, near_r, x_s, x_r, q_s, q_r, wi_s, wi_r, wo_s, wo_r,
@@ -370,6 +370,8 @@
         for d in range(1, nmp):
             square_copy(d, c).start()
 
+    gains = gain_ref[...].astype(f32).reshape(1, width)
+
     def normalize(c):
         here = slice(c * size, (c + 1) * size)
         for d in range(1, nmp):
@@ -384,7 +386,7 @@
         inverse = lax.rsqrt(square / (width * nmp) + epsilon)
         column = jnp.broadcast_to(inverse[0:1, 0:size], (128, size)).T[:, 0:1]
         normed[here, :] = (
-            state[here, :].astype(f32) * column * gain_ref[...].astype(f32)
+            state[here, :].astype(f32) * column * gains
         ).astype(bf16)
 
     def own_rows(c):
@@ -524,7 +526,7 @@
             contrib[c, z] += from_above[c, z].astype(f32)
 
         here = pl.ds(c * size, size)
-        out_ref[here, :] = (state[here, :].astype(f32) + contrib[c, z]).astype(bf16)
+        delta_ref[here, :] = contrib[c, z]
 
     hot[...] = jnp.zeros_like(hot)
     eager = min(2, count)
@@ -576,7 +578,7 @@
     for d in range(1, ny):
         mean_copy(d).wait_recv()
         total = total + hot_other[d - 1, 0:1, :]
-    mean_ref[...] = total / total_tokens
+    mean_ref[...] = total
 
     for c in range(count):
         for k in range(nz - 1):
@@ -647,14 +649,15 @@
     bf16 = jnp.bfloat16
     return pl.pallas_call(
         functools.partial(
-            layer_kernel, nz, ny, nmp, up, window, per, count, HEAD_DIM ** (-0.5), n * rows
+            layer_kernel, nz, ny, nmp, up, window, per, count, HEAD_DIM ** (-0.5)
         ),
         out_shape=[
             jax.ShapeDtypeStruct((rows, width), bf16),
+            jax.ShapeDtypeStruct((rows, width), f32),
             jax.ShapeDtypeStruct((1, slots), f32),
         ],
         in_specs=[vmem] * 7 + [pl.BlockSpec(memory_space=pltpu.SMEM)] + [anywhere] * 3,
-        out_specs=[vmem, vmem],
+        out_specs=[vmem, vmem, vmem],
         scratch_shapes=[
             VMEM((window, rows, width), bf16),
             VMEM((window, rows, width), bf16),
@@ -674,7 +677,6 @@
             VMEM((rows, width), bf16),
             VMEM((rows, width), f32),
             VMEM((count, nmp, 8, 128), f32),
-            VMEM((rows, width), bf16),
             VMEM((rows, width), bf16),
             VMEM((count, nz, size, width), bf16),
             VMEM((count, span, wide), bf16),
@@ -726,7 +728,7 @@
             collective_id=collective_id, has_side_effects=True, vmem_limit_bytes=67043328
         ),
     )(
-        queries, keys, values, doc_ids[None, :], resid, gain[None, :], index, live, w_in.T, w_out, out_proj,
+        queries, keys, values, doc_ids[None, :], resid, gain, index, live, w_in.T, w_out, out_proj,
     )
 
 
@@ -744,9 +746,11 @@
     hot_index,
     hot_blocks,
 ):
-    return layer(
+    state, delta, sums = layer(
         queries, keys, values, doc_ids, resid, ffn_gain, hot_index, hot_blocks, w_in, w_out, out_proj, ny, 4, 0
     )
+    total_tokens = resid.shape[0] * lax.axis_size("seq")
+    return (state.astype(jnp.float32) + delta).astype(jnp.bfloat16), sums / total_tokens
 
 
 def solution(mesh):

time: 181 us -> 180 us (level)
  local copies, waits for them, and re-layouts: 4.47 us -> 0.01 us
  other arithmetic: 0 us -> 3 us
    unnamed x2, local copies, waits for them, and re-layouts: 3.19 us -> 0.01 us
    convert_element_type x0 -> x1, other arithmetic: none -> 2.43 us  [local(): (state.astype(jnp.float32) + delta).astype(jnp.bfloat16)]
where the time goes in v5:
time: 180 us
  Pallas kernels  176 us (98%)
  other arithmetic  3 us (2%)
    pallas_call x1, Pallas kernels, layer(): pl.pallas_call(functools.partial(layer_kernel, nz, ny, nmp, up, window, p...  176 us

profile of v5, /device:TPU:0, one launch (start us, length us, event | category | flops | bytes accessed | tf_op | source)
XLA Modules:
  0.0 179.8 jit_solution(3317289347118641758)
XLA Ops:
  1.3 175.5 %shard_map.122 = (bf16[256,1280]{1,0:T(8,128)(2,1)}, f32[256,1280]{1,0:T(8,128)}, f32[1,384]{1,0:T(1,128)}) custom-call(bf16[256,1280]{1,0:T(8,128)(2,1)} %q_ref.1, bf16[256,1280]{1,0:T(8,128)(2,1)} %k_ref.1, bf16[256,1280]{1,0:T(8,128)(2,1)} %v_ref.1, s32[1,256]{1,0:T(1,128)} %bitcast.3, bf16[256,1280]{1,0:T(8,128)(2,1)} %resid_ref.1, ...), custom_call_target="tpu_custom_call" | custom-call | tf_op jit(solution)/shard_map/pallas_call | solution.py:650
  176.8 0.0 copy-start
  176.8 2.4 %add_convert_fusion = bf16[256,1280]{1,0:T(8,128)(2,1)} fusion(f32[256,1280]{1,0:T(8,128)} %get-tuple-element.6, bf16[256,1280]{1,0:T(8,128)(2,1)} %get-tuple-element.5), kind=kLoop, calls=%fused_computation | loop fusion | flops 983040 | bytes 2621440 | tf_op jit(solution)/shard_map/convert_element_type | solution.py:753
  179.3 0.0 copy-done
  179.3 0.6 broadcast_multiply_fusion
Async XLA Ops:
  176.8 2.4 %copy-start = (f32[1,384]{1,0:T(1,128)S(1)}, f32[1,384]{1,0:T(1,128)}, u32[]{:S(2)}) copy-start(f32[1,384]{1,0:T(1,128)} %get-tuple-element.7) | copy-start | bytes 4612
